TPU v7x, 8 devices: a whole 2x2x1 slice. The times are simulated.
8 devices in a mesh: dp: 2 (over z, y), pp: 4 (over x, core).
Axes of the slice: x: 2, y: 2, z: 1, core: 2. Of those that a mesh axis runs over, the one named last changes fastest.
Arguments:
- x_embed: bfloat16 [24, 512, 512], P('dp'), parts along dimension 0
- labels: int32 [24, 512], P('dp'), parts along dimension 0
- norm_gain: float32 [4, 2, 1, 512], P('pp')
- w_up: bfloat16 [4, 2, 1, 512, 2048], P('pp')
- w_down: bfloat16 [4, 2, 1, 2048, 512], P('pp')
- w_head: bfloat16 [50304, 512], P('pp')
Outputs:
- output 1: float32 [2], P('dp'), parts along dimension 0
- output 2: float32 [24, 512, 512], P(('dp', 'pp')), parts along dimension 0
- output 3: float32 [8, 2, 1, 512], P(('dp', 'pp')), parts along dimension 0
- output 4: bfloat16 [8, 2, 1, 512, 2048], P(('dp', 'pp')), parts along dimension 0
- output 5: bfloat16 [8, 2, 1, 2048, 512], P(('dp', 'pp')), parts along dimension 0
- output 6: bfloat16 [100608, 512], P(('dp', 'pp')), parts along dimension 0
There are 2 independent parts. A program takes and returns all parts, laid end to end along the dimension named above; an argument that names none is the same for every part.
All inputs are finite; a program needn't handle non-finite values.
Results may differ from a plain program's by a relative error of at most 0.02.
Values are sent between devices in bfloat16 or wider.
A program may use at most 1 GiB of HBM per device.

v0:
```python
import jax
import jax.numpy as jnp
from jax import lax
from jax.sharding import PartitionSpec as P

NORM_EPS = 1e-6


def rms_scale(h_f32):
    return lax.rsqrt(jnp.mean(h_f32 * h_f32, axis=-1, keepdims=True) + NORM_EPS)


def gain_norm(h_f32, gain_vec):
    return h_f32 * rms_scale(h_f32) * gain_vec


def plain_norm(h_f32):
    return h_f32 * rms_scale(h_f32)


def contract_last(lhs_mat, rhs_mat):
    return lax.dot_general(lhs_mat, rhs_mat, (((1,), (1,)), ((), ())), preferred_element_type=jnp.float32)


def contract_first(lhs_mat, rhs_mat):
    return lax.dot_general(lhs_mat, rhs_mat, (((0,), (0,)), ((), ())), preferred_element_type=jnp.float32)


def take_row(buffer, row_id):
    return lax.dynamic_index_in_dim(buffer, row_id, 0, False)


def masked_store(buffer, new_value, row_id, keep_mask):
    prev_value = take_row(buffer, row_id)
    return lax.dynamic_update_index_in_dim(buffer, jnp.where(keep_mask, new_value, prev_value), row_id, 0)


def add_row(buffer, delta, row_id):
    return lax.dynamic_update_index_in_dim(buffer, take_row(buffer, row_id) + delta, row_id, 0)


def slot_of(offset, num_micro, n_stage):
    is_valid = (offset >= 0) & (offset < 2 * num_micro)
    clipped = jnp.clip(offset, 0, 2 * num_micro - 1)
    within = clipped % (2 * n_stage)
    micro_id = (clipped // (2 * n_stage)) * n_stage + within % n_stage
    return is_valid, within // n_stage, micro_id


def block_inner(h_in, gain_vec, w_up):
    normed = gain_norm(h_in.astype(jnp.float32), gain_vec).astype(jnp.bfloat16)
    pre_act = jnp.dot(normed, w_up, preferred_element_type=jnp.float32)
    hidden = jax.nn.gelu(pre_act).astype(jnp.bfloat16)
    return normed, pre_act, hidden


def block_output(h_in, hidden, w_down):
    return (h_in.astype(jnp.float32) + jnp.dot(hidden, w_down, preferred_element_type=jnp.float32)).astype(jnp.bfloat16)


def block_backward(d_out, h_in, normed, pre_act, hidden, gain_vec, w_up, w_down):
    d_out_b = d_out.astype(jnp.bfloat16)
    d_hidden = contract_last(d_out_b, w_down)
    grad_down = contract_first(hidden, d_out_b)
    gelu_pull = jax.vjp(jax.nn.gelu, pre_act)[1]
    d_pre = gelu_pull(d_hidden)[0].astype(jnp.bfloat16)
    grad_up = contract_first(normed, d_pre)
    d_normed = contract_last(d_pre, w_up)
    norm_pull = jax.vjp(gain_norm, h_in.astype(jnp.float32), gain_vec)[1]
    d_h_norm, grad_gain = norm_pull(d_normed)
    return d_out + d_h_norm, grad_gain, grad_up, grad_down


def run_forward(x_embed, stage_id, n_stage, layer_gains, layer_ups, layer_downs):
    num_micro, tokens, d_model = x_embed.shape
    stage_layers = layer_ups.shape[1]
    to_next = [(src, (src + 1) % n_stage) for src in range(n_stage)]
    is_first = stage_id == 0
    is_last = stage_id == n_stage - 1

    def fwd_step(step_num, loop_state):
        act_carry, saved_in, final_h = loop_state
        is_valid, half_id, micro_id = slot_of(step_num - stage_id, num_micro, n_stage)
        h_cur = jnp.where(is_first & (half_id == 0), take_row(x_embed, micro_id), act_carry)
        saved_in = masked_store(saved_in, h_cur, half_id * num_micro + micro_id, is_valid)
        half_gains = take_row(layer_gains, half_id)
        half_ups = take_row(layer_ups, half_id)
        half_downs = take_row(layer_downs, half_id)
        for layer_id in range(stage_layers):
            hidden = block_inner(h_cur, half_gains[layer_id], half_ups[layer_id])[2]
            h_cur = block_output(h_cur, hidden, half_downs[layer_id])
        final_h = masked_store(final_h, h_cur, micro_id, is_valid & is_last & (half_id == 1))
        act_carry = lax.ppermute(h_cur, 'pp', to_next)
        return act_carry, saved_in, final_h

    init_state = (jnp.zeros((tokens, d_model), jnp.bfloat16), jnp.zeros((2 * num_micro, tokens, d_model), jnp.bfloat16), jnp.zeros((num_micro, tokens, d_model), jnp.bfloat16))
    end_state = lax.fori_loop(0, 2 * num_micro + n_stage - 1, fwd_step, init_state)
    return end_state[1], end_state[2]


def run_head(final_h, labels, w_head, stage_id, n_stage):
    num_micro, tokens, d_model = final_h.shape
    vocab_local = w_head.shape[0]
    is_last = stage_id == n_stage - 1
    inv_count = 1.0 / (num_micro * tokens)
    vocab_ids = lax.broadcasted_iota(jnp.int32, (1, vocab_local), 1) + stage_id * vocab_local

    def head_step(micro_id, loop_state):
        loss_acc, head_grad, d_final = loop_state
        h_f32 = take_row(final_h, micro_id).astype(jnp.float32)
        h_norm = plain_norm(h_f32).astype(jnp.bfloat16)
        h_norm = lax.psum(jnp.where(is_last, h_norm, jnp.zeros_like(h_norm)), 'pp')
        logits = contract_last(h_norm, w_head)
        label_hit = vocab_ids == take_row(labels, micro_id)[:, None]
        row_max = lax.pmax(jnp.max(logits, axis=-1), 'pp')
        exp_shift = jnp.exp(logits - row_max[:, None])
        tok_stats = lax.psum(jnp.stack([jnp.sum(exp_shift, axis=-1), jnp.sum(jnp.where(label_hit, logits, 0.0), axis=-1)]), 'pp')
        loss_acc = loss_acc + jnp.sum(row_max + jnp.log(tok_stats[0]) - tok_stats[1]) * inv_count
        d_logits = ((exp_shift / tok_stats[0][:, None] - label_hit.astype(jnp.float32)) * inv_count).astype(jnp.bfloat16)
        head_grad = head_grad + contract_first(d_logits, h_norm)
        d_norm = lax.psum(jnp.dot(d_logits, w_head, preferred_element_type=jnp.float32), 'pp')
        norm_pull = jax.vjp(plain_norm, h_f32)[1]
        d_final = masked_store(d_final, norm_pull(d_norm)[0].astype(jnp.bfloat16), micro_id, is_last)
        return loss_acc, head_grad, d_final

    init_state = (jnp.zeros((), jnp.float32), jnp.zeros((vocab_local, d_model), jnp.float32), jnp.zeros((num_micro, tokens, d_model), jnp.bfloat16))
    return lax.fori_loop(0, num_micro, head_step, init_state)


def run_backward(saved_in, d_final, stage_id, n_stage, layer_gains, layer_ups, layer_downs):
    num_micro, tokens, d_model = d_final.shape
    stage_layers = layer_ups.shape[1]
    to_prev = [(src, (src - 1) % n_stage) for src in range(n_stage)]
    is_first = stage_id == 0
    is_last = stage_id == n_stage - 1

    def bwd_step(step_num, loop_state):
        grad_carry, acc_gain, acc_up, acc_down, d_embed = loop_state
        is_valid, rev_half, micro_id = slot_of(step_num - (n_stage - 1 - stage_id), num_micro, n_stage)
        half_id = 1 - rev_half
        d_cur = jnp.where(is_last & (half_id == 1), take_row(d_final, micro_id), grad_carry).astype(jnp.float32)
        d_cur = jnp.where(is_valid, d_cur, 0.0)
        h_cur = take_row(saved_in, half_id * num_micro + micro_id)
        half_gains = take_row(layer_gains, half_id)
        half_ups = take_row(layer_ups, half_id)
        half_downs = take_row(layer_downs, half_id)
        records = []
        for layer_id in range(stage_layers):
            inner_vals = block_inner(h_cur, half_gains[layer_id], half_ups[layer_id])
            records.append((h_cur,) + inner_vals)
            if layer_id + 1 < stage_layers:
                h_cur = block_output(h_cur, inner_vals[2], half_downs[layer_id])
        gain_parts = []
        up_parts = []
        down_parts = []
        for layer_id in reversed(range(stage_layers)):
            saved_rec = records[layer_id]
            d_cur, grad_gain, grad_up, grad_down = block_backward(d_cur, saved_rec[0], saved_rec[1], saved_rec[2], saved_rec[3], half_gains[layer_id], half_ups[layer_id], half_downs[layer_id])
            gain_parts.insert(0, grad_gain)
            up_parts.insert(0, grad_up)
            down_parts.insert(0, grad_down)
        acc_gain = add_row(acc_gain, jnp.stack(gain_parts), half_id)
        acc_up = add_row(acc_up, jnp.stack(up_parts), half_id)
        acc_down = add_row(acc_down, jnp.stack(down_parts), half_id)
        d_embed = masked_store(d_embed, d_cur, micro_id, is_valid & is_first & (half_id == 0))
        grad_carry = lax.ppermute(d_cur.astype(jnp.bfloat16), 'pp', to_prev)
        return grad_carry, acc_gain, acc_up, acc_down, d_embed

    init_state = (jnp.zeros((tokens, d_model), jnp.bfloat16), jnp.zeros(layer_gains.shape, jnp.float32), jnp.zeros(layer_ups.shape, jnp.float32), jnp.zeros(layer_downs.shape, jnp.float32), jnp.zeros((num_micro, tokens, d_model), jnp.float32))
    end_state = lax.fori_loop(0, 2 * num_micro + n_stage - 1, bwd_step, init_state)
    return end_state[1], end_state[2], end_state[3], end_state[4]


def solution(mesh):
    n_stage = mesh.shape['pp']

    def local_step(x_embed, labels, norm_gain, w_up, w_down, w_head):
        stage_id = lax.axis_index('pp')
        layer_gains = norm_gain[0]
        layer_ups = w_up[0]
        layer_downs = w_down[0]
        saved_in, final_h = run_forward(x_embed, stage_id, n_stage, layer_gains, layer_ups, layer_downs)
        loss_acc, head_grad, d_final = run_head(final_h, labels, w_head, stage_id, n_stage)
        acc_gain, acc_up, acc_down, d_embed = run_backward(saved_in, d_final, stage_id, n_stage, layer_gains, layer_ups, layer_downs)
        d_embed = lax.psum_scatter(d_embed, 'pp', scatter_dimension=0, tiled=True)
        return (loss_acc.reshape(1), d_embed, acc_gain[None], acc_up.astype(jnp.bfloat16)[None], acc_down.astype(jnp.bfloat16)[None], head_grad.astype(jnp.bfloat16))

    part_spec = P('dp')
    stage_spec = P('pp')
    out_spec = P(('dp', 'pp'))
    return jax.shard_map(local_step, mesh=mesh, in_specs=(part_spec, part_spec, stage_spec, stage_spec, stage_spec, stage_spec), out_specs=(part_spec, out_spec, out_spec, out_spec, out_spec, out_spec), check_vma=False)
```

profile of v0, /device:TPU:0, one launch (start us, length us, event | category | flops | bytes accessed | tf_op | source)
XLA Modules:
  0.0 3259.2 jit_solution(3712872867898479874)
XLA Ops:
  17.2 486.0 %while.62 = (s32[]{:T(128)}, bf16[512,512]{1,0:T(8,128)(2,1)S(1)}, bf16[24,512,512]{2,1,0:T(8,128)(2,1)}, bf16[12,512,512]{2,1,0:T(8,128)(2,1)}, s32[]{:T(128)},...) while((s32[]{:T(128)}, bf16[512,512]{1,0:T(8,128)(2,1)S(1)}, ...), condition=%wide.region_2.3_spmd, body=%wide.region_0.2_spmd.sunk | while | flops 2160329216 | bytes 14172951 | solution.py:97
  506.3 1622.9 %while.64 = (s32[]{:T(128)}, f32[]{:T(128)}, f32[12576,512]{1,0:T(8,128)}, bf16[12,512,512]{2,1,0:T(8,128)(2,1)}, pred[]{:T(512)}, /*index=5*/bf16[12,512,512]{2...) while((s32[]{:T(128)}, f32[]{:T(128)}, ...), condition=%wide.region_14.15_spmd.clone, body=%wide.region_3.14_spmd.clone.sunk | while | flops 19881922560 | bytes 265353408 | solution.py:127
  511.6 28.0 all-reduce.4.cloned.1.call-done
  539.6 14.9 fusion.190
  607.3 21.6 select_add_fusion.2
  648.4 26.4 all-reduce.4.cloned.1.call-done
  674.8 14.9 fusion.190
  742.5 26.7 select_add_fusion.2
  783.5 26.1 all-reduce.4.cloned.1.call-done
  809.6 14.9 fusion.190
  877.3 26.7 select_add_fusion.2
  918.3 26.4 all-reduce.4.cloned.1.call-done
  1012.4 26.7 select_add_fusion.2
  1053.5 26.4 all-reduce.4.cloned.1.call-done
  1080.0 14.9 fusion.190
  1147.7 26.7 select_add_fusion.2
  1188.7 26.4 all-reduce.4.cloned.1.call-done
  1282.8 26.7 select_add_fusion.2
  1323.9 26.4 all-reduce.4.cloned.1.call-done
  1418.0 26.7 select_add_fusion.2
  1459.1 26.2 all-reduce.4.cloned.1.call-done
  1553.0 26.7 select_add_fusion.2
  1594.0 26.1 all-reduce.4.cloned.1.call-done
  1687.9 26.7 select_add_fusion.2
  1728.9 26.4 all-reduce.4.cloned.1.call-done
  1823.0 26.7 select_add_fusion.2
  1864.1 26.4 all-reduce.4.cloned.1.call-done
  1958.3 26.7 select_add_fusion.2
  1999.3 26.4 all-reduce.4.cloned.1.call-done
  2093.4 26.7 select_add_fusion.2
  2144.0 1015.6 %while.63 = (s32[]{:T(128)}, bf16[512,512]{1,0:T(8,128)(2,1)S(1)}, f32[2,1,512]{2,1,0:T(1,128)S(1)}, f32[2,1,512,2048]{3,2,1,0:T(8,128)}, f32[2,1,2048,512]{3,2,...) while((s32[]{:T(128)}, bf16[512,512]{1,0:T(8,128)(2,1)S(1)}, ...), condition=%wide.region_19.20_spmd, body=%wide.region_15.19_spmd.sunk | while | flops 5413014528 | bytes 151047184 | solution.py:170
  3184.2 66.4 %reduce-scatter.4.cloned.1.call-done = f32[3,512,512]{2,1,0:T(8,128)} async-done(((f32[12,512,512]{2,1,0:T(8,128)}), f32[3,512,512]{2,1,0:T(8,128)}) %reduce-scatter.4.cloned.1.call-update) | async-done | bytes 3145744
  (1315 shorter events, 2468.8 us)
Async XLA Ops:
  506.3 33.3 %all-reduce.4.cloned.1.call-start = ((), (), s32[]{:S(2)}) async-start(), calls=%async_computation.2 | async-start | bytes 1048576 | tf_op jit(solution)/shard_map/while/body/eval_jaxpr/psum | solution.py:112
  509.6 129.4 %all-reduce.6.cloned.1.call-start = ((), (), s32[]{:S(2)}) async-start(), calls=%async_computation.3 | async-start | bytes 2097152 | tf_op jit(solution)/shard_map/while/body/eval_jaxpr/psum | solution.py:121
  643.1 31.7 all-reduce.4.cloned.1.call-start
  646.3 127.8 %all-reduce.6.cloned.1.call-start = ((), (), s32[]{:S(2)}) async-start(), calls=%async_computation.3 | async-start | bytes 2097152 | tf_op jit(solution)/shard_map/while/body/eval_jaxpr/psum | solution.py:121
  778.2 31.4 all-reduce.4.cloned.1.call-start
  781.5 127.5 %all-reduce.6.cloned.1.call-start = ((), (), s32[]{:S(2)}) async-start(), calls=%async_computation.3 | async-start | bytes 2097152 | tf_op jit(solution)/shard_map/while/body/eval_jaxpr/psum | solution.py:121
  913.0 31.7 all-reduce.4.cloned.1.call-start
  916.3 127.8 %all-reduce.6.cloned.1.call-start = ((), (), s32[]{:S(2)}) async-start(), calls=%async_computation.3 | async-start | bytes 2097152 | tf_op jit(solution)/shard_map/while/body/eval_jaxpr/psum | solution.py:121
  1048.2 31.8 all-reduce.4.cloned.1.call-start
  1051.5 127.9 %all-reduce.6.cloned.1.call-start = ((), (), s32[]{:S(2)}) async-start(), calls=%async_computation.3 | async-start | bytes 2097152 | tf_op jit(solution)/shard_map/while/body/eval_jaxpr/psum | solution.py:121
  1183.4 31.7 all-reduce.4.cloned.1.call-start
  1186.7 127.9 %all-reduce.6.cloned.1.call-start = ((), (), s32[]{:S(2)}) async-start(), calls=%async_computation.3 | async-start | bytes 2097152 | tf_op jit(solution)/shard_map/while/body/eval_jaxpr/psum | solution.py:121
  1318.6 31.8 all-reduce.4.cloned.1.call-start
  1321.9 127.9 %all-reduce.6.cloned.1.call-start = ((), (), s32[]{:S(2)}) async-start(), calls=%async_computation.3 | async-start | bytes 2097152 | tf_op jit(solution)/shard_map/while/body/eval_jaxpr/psum | solution.py:121
  1453.8 31.5 all-reduce.4.cloned.1.call-start
  1457.1 127.6 %all-reduce.6.cloned.1.call-start = ((), (), s32[]{:S(2)}) async-start(), calls=%async_computation.3 | async-start | bytes 2097152 | tf_op jit(solution)/shard_map/while/body/eval_jaxpr/psum | solution.py:121
  1588.7 31.4 all-reduce.4.cloned.1.call-start
  1592.0 127.6 %all-reduce.6.cloned.1.call-start = ((), (), s32[]{:S(2)}) async-start(), calls=%async_computation.3 | async-start | bytes 2097152 | tf_op jit(solution)/shard_map/while/body/eval_jaxpr/psum | solution.py:121
  1723.6 31.7 all-reduce.4.cloned.1.call-start
  1726.9 127.9 %all-reduce.6.cloned.1.call-start = ((), (), s32[]{:S(2)}) async-start(), calls=%async_computation.3 | async-start | bytes 2097152 | tf_op jit(solution)/shard_map/while/body/eval_jaxpr/psum | solution.py:121
  1858.8 31.8 all-reduce.4.cloned.1.call-start
  1862.1 127.8 %all-reduce.6.cloned.1.call-start = ((), (), s32[]{:S(2)}) async-start(), calls=%async_computation.3 | async-start | bytes 2097152 | tf_op jit(solution)/shard_map/while/body/eval_jaxpr/psum | solution.py:121
  1994.0 31.7 all-reduce.4.cloned.1.call-start
  1997.3 127.8 %all-reduce.6.cloned.1.call-start = ((), (), s32[]{:S(2)}) async-start(), calls=%async_computation.3 | async-start | bytes 2097152 | tf_op jit(solution)/shard_map/while/body/eval_jaxpr/psum | solution.py:121
  2129.2 1121.5 %reduce-scatter.4.cloned.1.call-start = ((), (), s32[]{:S(2)}) async-start(), calls=%async_computation.1 | async-start | bytes 15728640
  2271.1 23.7 collective-permute-start.1
  2421.7 23.5 collective-permute-start.1
  2572.2 23.7 collective-permute-start.1
  2722.9 23.4 collective-permute-start.1
  2798.1 23.2 collective-permute-start.1
  2873.3 23.5 collective-permute-start.1
  3023.9 23.3 collective-permute-start.1
  (210 other events, 1434.4 us)
Sparse Core Ops, SparseCore 0:
  510.0 29.5 all-reduce.3
  607.4 31.5 all-reduce.5
  646.8 27.9 all-reduce.3
  742.6 31.5 all-reduce.5
  781.6 27.9 all-reduce.3
  877.4 31.5 all-reduce.5
  916.7 27.9 all-reduce.3
  1012.5 31.5 all-reduce.5
  1051.9 28.0 all-reduce.3
  1147.8 31.5 all-reduce.5
  1187.1 27.9 all-reduce.3
  1282.9 31.5 all-reduce.5
  1322.3 27.9 all-reduce.3
  1418.2 31.5 all-reduce.5
  1457.2 28.0 all-reduce.3
  1553.1 31.5 all-reduce.5
  1592.1 27.9 all-reduce.3
  1688.0 31.5 all-reduce.5
  1727.3 27.9 all-reduce.3
  1823.1 31.5 all-reduce.5
  1862.5 28.0 all-reduce.3
  1958.4 31.5 all-reduce.5
  1997.7 27.9 all-reduce.3
  2093.5 31.5 all-reduce.5
Sparse Core Ops, SparseCore 1:
  3159.7 90.8 reduce-scatter.3
where the time goes:
time: 3280 us; the launch traced here: 3260 us
  matrix products  1330 us (41%)
  other arithmetic  687 us (21%)
  waiting for transfers between devices  667 us (20%)
  local copies, waits for them, and re-layouts  395 us (12%)
  blocking collectives  138 us (4%)
    dot_general x66, matrix products, contract_first(): lax.dot_general(lhs_mat, rhs_mat, (((0,), (0,)), ((), ())), preferred_ele...  598 us
    dot_general x66, matrix products, contract_last(): lax.dot_general(lhs_mat, rhs_mat, (((1,), (1,)), ((), ())), preferred_ele...  353 us
    psum x12, waiting for transfers between devices, head_step(): h_norm = lax.psum(jnp.where(is_last, h_norm, jnp.zeros_like(h_norm)), 'pp')  318 us
    dynamic_slice x186, local copies, waits for them, and re-layouts, take_row(): return lax.dynamic_index_in_dim(buffer, row_id, 0, False)  289 us
    ppermute x27, waiting for transfers between devices, fwd_step(): act_carry = lax.ppermute(h_cur, 'pp', to_next)  232 us
    dynamic_update_slice x66, other arithmetic, masked_store(): lax.dynamic_update_index_in_dim(buffer, jnp.where(keep_mask, new_value, p...  156 us
    convert_element_type x12, other arithmetic, head_step(): ((exp_shift / tok_stats[0][:, None] - label_hit.astype(jnp.float32)) * in...  156 us
    dot_general x27, matrix products, block_output(): jnp.dot(hidden, w_down, preferred_element_type=jnp.float32)  156 us
  transfers between devices with their start and end apart: 79, of which 52 were waited for; matrix products, arithmetic and copies ran while one was open for 29% of the time, Pallas kernels for 0%

commit v1 on v0

v1 whole, which is shorter than its diff:
```python
import functools

import jax
import jax.numpy as jnp
from jax import lax
from jax.experimental import pallas as pl
from jax.experimental.pallas import tpu as pltpu
from jax.sharding import PartitionSpec as P

NORM_EPS = 1e-6
VMEM_MAX = 67_000_000
GELU_A = 0.7978845608028654
GELU_B = GELU_A * 0.044715
SUB = 1024

ANY = pl.BlockSpec(memory_space=pl.ANY)
VMEM = pl.BlockSpec(memory_space=pltpu.VMEM)


def nn(lhs, rhs):
    return lax.dot_general(lhs, rhs, (((1,), (0,)), ((), ())), preferred_element_type=jnp.float32)


def nt(lhs, rhs):
    return lax.dot_general(lhs, rhs, (((1,), (1,)), ((), ())), preferred_element_type=jnp.float32)


def col_scale(h_f32):
    return lax.rsqrt(jnp.mean(h_f32 * h_f32, axis=0, keepdims=True) + NORM_EPS)


def gelu_pair(x):
    x2 = x * x
    th = jnp.tanh(x * (GELU_A + GELU_B * x2))
    hx = 0.5 * x
    slope = 0.5 + 0.5 * th + hx * (1.0 - th * th) * (GELU_A + (3.0 * GELU_B) * x2)
    return hx + hx * th, slope


def group_barrier(me, n_stage):
    sem = pltpu.get_barrier_semaphore()
    for step in range(1, n_stage):
        pl.semaphore_signal(sem, inc=1, device_id={"pp": lax.rem(me + step, n_stage)}, device_id_type=pl.DeviceIdType.MESH)
    pl.semaphore_wait(sem, n_stage - 1)


def remote(src, dst, send_sem, recv_sem, dev):
    return pltpu.make_async_remote_copy(src_ref=src, dst_ref=dst, send_sem=send_sem, recv_sem=recv_sem, device_id={"pp": dev}, device_id_type=pl.DeviceIdType.MESH)


def fwd_kernel(n_stage, num_micro, x_ref, g_ref, w1t_ref, w2t_ref, saved_ref, slope_ref, hid_ref, hfin_ref,
               hbuf, obuf, fbuf, slope_st, hid_st, in_sem, out_sem, save_sem, slope_sem, hid_sem, fin_sem, fin_a, fin_b, fin_c):
    me = lax.axis_index("pp")
    right = lax.rem(me + 1, n_stage)
    first, last = me == 0, me == n_stage - 1
    n_unit = 2 * num_micro
    d_ff = w1t_ref.shape[1]
    group_barrier(me, n_stage)

    @pl.when(first)
    def _():
        @pl.loop(0, num_micro)
        def _(m):
            pltpu.make_async_copy(x_ref.at[m], hbuf.at[m], in_sem.at[m]).start()

    @pl.loop(0, n_unit)
    def _(u):
        half = u // num_micro
        m = lax.rem(u, num_micro)
        from_x = first & (half == 0)
        is_final = last & (half == 1)
        par = lax.rem(u, 2)

        @pl.when(from_x)
        def _():
            pltpu.make_async_copy(x_ref.at[m], hbuf.at[u], in_sem.at[u]).wait()

        @pl.when(jnp.logical_not(from_x))
        def _():
            remote(obuf.at[0], hbuf.at[u], out_sem.at[0], in_sem.at[u], right).wait_recv()

        pltpu.make_async_copy(hbuf.at[u], saved_ref.at[u], save_sem.at[u]).start()

        @pl.when(u >= 2)
        def _():
            pltpu.make_async_copy(slope_st.at[par], slope_ref.at[u - 2], slope_sem.at[par]).wait()
            pltpu.make_async_copy(hid_st.at[par], hid_ref.at[u - 2], hid_sem.at[par]).wait()

        h = hbuf[u].astype(jnp.float32)
        y = (h * col_scale(h) * g_ref[half]).astype(jnp.bfloat16)
        step = 512
        for k in range(d_ff // step):
            rows = pl.ds(k * step, step)
            hid, slope = gelu_pair(nn(w1t_ref[half, rows, :], y))
            hid_st[par, rows, :] = hid.astype(jnp.bfloat16)
            slope_st[par, rows, :] = slope
        out = (h + nn(w2t_ref[half], hid_st[par])).astype(jnp.bfloat16)
        pltpu.make_async_copy(slope_st.at[par], slope_ref.at[u], slope_sem.at[par]).start()
        pltpu.make_async_copy(hid_st.at[par], hid_ref.at[u], hid_sem.at[par]).start()

        @pl.when(is_final)
        def _():
            fbuf[m] = out
            pltpu.make_async_copy(fbuf.at[m], hfin_ref.at[m], fin_c.at[m]).start()
            remote(fbuf.at[m], hfin_ref.at[m], fin_a.at[m], fin_sem.at[m], n_stage - 2).start()
            remote(fbuf.at[m], hfin_ref.at[m], fin_b.at[m], fin_sem.at[m], 1).start()

        @pl.when(jnp.logical_not(is_final))
        def _():
            slot = lax.rem(u, 4)

            @pl.when(u >= 4)
            def _():
                remote(obuf.at[slot], hbuf.at[u], out_sem.at[slot], in_sem.at[u], right).wait_send()

            obuf[slot] = out
            dst = u + jnp.where(last, num_micro, 0)
            remote(obuf.at[slot], hbuf.at[dst], out_sem.at[slot], in_sem.at[dst], right).start()

    for slot in range(4):
        remote(obuf.at[slot], hbuf.at[0], out_sem.at[slot], in_sem.at[0], right).wait_send()
    for par in range(2):
        pltpu.make_async_copy(slope_st.at[par], slope_ref.at[par], slope_sem.at[par]).wait()
        pltpu.make_async_copy(hid_st.at[par], hid_ref.at[par], hid_sem.at[par]).wait()

    @pl.loop(0, n_unit)
    def _(u):
        pltpu.make_async_copy(hbuf.at[u], saved_ref.at[u], save_sem.at[u]).wait()

    @pl.when(last)
    def _():
        @pl.loop(0, num_micro)
        def _(m):
            pltpu.make_async_copy(fbuf.at[m], hfin_ref.at[m], fin_c.at[m]).wait()
            remote(fbuf.at[m], hfin_ref.at[m], fin_a.at[m], fin_sem.at[m], n_stage - 2).wait_send()
            remote(fbuf.at[m], hfin_ref.at[m], fin_b.at[m], fin_sem.at[m], 1).wait_send()

    @pl.when(jnp.logical_not(last))
    def _():
        @pl.loop(0, num_micro)
        def _(m):
            remote(fbuf.at[m], hfin_ref.at[m], fin_a.at[m], fin_sem.at[m], right).wait_recv()

            @pl.when(me == 1)
            def _():
                remote(hfin_ref.at[m], hfin_ref.at[m], fin_a.at[m], fin_sem.at[m], 0).start()

    @pl.when(me == 1)
    def _():
        @pl.loop(0, num_micro)
        def _(m):
            remote(hfin_ref.at[m], hfin_ref.at[m], fin_a.at[m], fin_sem.at[m], 0).wait_send()


def run_forward(x_t, gains, w1t, w2t, n_stage):
    num_micro, d_model, tokens = x_t.shape
    d_ff = w1t.shape[1]
    bf, f32 = jnp.bfloat16, jnp.float32
    n_unit = 2 * num_micro
    dma = pltpu.SemaphoreType.DMA
    return pl.pallas_call(
        functools.partial(fwd_kernel, n_stage, num_micro),
        name="stack_fwd",
        out_shape=(jax.ShapeDtypeStruct((n_unit, d_model, tokens), bf), jax.ShapeDtypeStruct((n_unit, d_ff, tokens), f32),
                   jax.ShapeDtypeStruct((n_unit, d_ff, tokens), bf), jax.ShapeDtypeStruct((num_micro, d_model, tokens), bf)),
        in_specs=[ANY, VMEM, VMEM, VMEM],
        out_specs=(ANY, ANY, ANY, ANY),
        scratch_shapes=[
            pltpu.VMEM((n_unit, d_model, tokens), bf), pltpu.VMEM((4, d_model, tokens), bf), pltpu.VMEM((num_micro, d_model, tokens), bf),
            pltpu.VMEM((2, d_ff, tokens), f32), pltpu.VMEM((2, d_ff, tokens), bf),
            dma((n_unit,)), dma((4,)), dma((n_unit,)), dma((2,)), dma((2,)), dma((num_micro,)), dma((num_micro,)), dma((num_micro,)), dma((num_micro,)),
        ],
        compiler_params=pltpu.CompilerParams(collective_id=0, has_side_effects=True, vmem_limit_bytes=VMEM_MAX),
        cost_estimate=pl.CostEstimate(flops=4 * n_unit * tokens * d_model * d_ff, bytes_accessed=7 * n_unit * d_ff * tokens, transcendentals=0),
    )(x_t, gains, w1t, w2t)


def sub_tiles(tile):
    n_sub = tile // SUB
    return [(k * SUB, SUB if k + 1 < n_sub else tile - k * SUB) for k in range(n_sub)]


def logits_kernel(h_ref, lab_ref, w_ref, e_ref, mrun_ref, stat_ref, n_ref, run):
    j = pl.program_id(1)
    tile = e_ref.shape[1]
    subs = sub_tiles(tile)

    @pl.when(j == 0)
    def _():
        run[0:1, :] = jnp.full((1, run.shape[1]), -jnp.inf, jnp.float32)
        run[1:3, :] = jnp.zeros((2, run.shape[1]), jnp.float32)
        h = h_ref[0].astype(jnp.float32)
        n_ref[0] = (h * col_scale(h)).astype(jnp.bfloat16)

    n = n_ref[0]
    lab = lab_ref[0] - j * tile
    m_run, s_run, z_lab = run[0:1, :], run[1:2, :], run[2:3, :]
    for k, (off, size) in enumerate(subs):
        z = nn(w_ref[pl.ds(pl.multiple_of(j * tile + off, 16), size), :], n)
        m_new = jnp.maximum(m_run, jnp.max(z, axis=0, keepdims=True))
        e = jnp.exp(z - m_new)
        e_ref[0, off:off + size, :] = e.astype(jnp.bfloat16)
        s_run = s_run * jnp.exp(m_run - m_new) + jnp.sum(e, axis=0, keepdims=True)
        hit = lax.broadcasted_iota(jnp.int32, z.shape, 0) == lab - off
        z_lab = z_lab + jnp.sum(jnp.where(hit, z, 0.0), axis=0, keepdims=True)
        m_run = m_new
        mrun_ref[0, pl.ds(j * len(subs) + k, 1), :] = m_run
    run[0:1, :] = m_run
    run[1:2, :] = s_run
    run[2:3, :] = z_lab
    stat_ref[0] = run[...]


def d_logits(e_tile, fac_row, lab, off, inv):
    hit = lax.broadcasted_iota(jnp.int32, e_tile.shape, 0) == lab - off
    return (e_tile.astype(jnp.float32) * fac_row - jnp.where(hit, inv, 0.0)).astype(jnp.bfloat16)


def dnorm_kernel(inv, e_ref, fac_ref, lab_ref, wt_ref, dn_ref):
    j = pl.program_id(1)
    tile = e_ref.shape[1]
    subs = sub_tiles(tile)
    lab = lab_ref[0] - j * tile
    total = None
    for k, (off, size) in enumerate(subs):
        d = d_logits(e_ref[0, off:off + size, :], fac_ref[0, pl.ds(j * len(subs) + k, 1), :], lab, off, inv)
        part = nn(wt_ref[j, :, off:off + size], d)
        total = part if total is None else total + part

    @pl.when(j == 0)
    def _():
        dn_ref[0] = total

    @pl.when(j > 0)
    def _():
        dn_ref[0] += total


def dhead_kernel(inv, e_ref, fac_ref, lab_ref, n_ref, out_ref, acc):
    j, i = pl.program_id(0), pl.program_id(1)
    tile = e_ref.shape[1]
    subs = sub_tiles(tile)
    per = e_ref.shape[0]

    @pl.when(i == 0)
    def _():
        acc[...] = jnp.zeros_like(acc)

    for k, (off, size) in enumerate(subs):
        total = None
        for b in range(per):
            d = d_logits(e_ref[b, off:off + size, :], fac_ref[b, pl.ds(j * len(subs) + k, 1), :], lab_ref[b] - j * tile, off, inv)
            part = nt(d, n_ref[b])
            total = part if total is None else total + part
        acc[off:off + size, :] += total

    @pl.when(i == pl.num_programs(1) - 1)
    def _():
        out_ref[...] = acc[...].astype(jnp.bfloat16)


def run_head(h_fin, labels, w_head, stage_id, n_stage):
    num_micro, d_model, tokens = h_fin.shape
    vocab = w_head.shape[0]
    n_tile = 3
    tile = vocab // n_tile
    n_row = 16
    bf, f32 = jnp.bfloat16, jnp.float32
    inv = 1.0 / (num_micro * tokens)
    lab = (labels - stage_id * vocab).reshape(num_micro, 1, tokens)
    params = pltpu.CompilerParams(vmem_limit_bytes=VMEM_MAX)
    flops = 2 * num_micro * tokens * d_model * vocab
    e_bytes = 2 * num_micro * tokens * vocab

    def cost(extra):
        return pl.CostEstimate(flops=flops, bytes_accessed=e_bytes + extra, transcendentals=0)

    micro3 = lambda shape: pl.BlockSpec(shape, lambda i, j: (i, 0, 0))
    e, m_run, stat, n_t = pl.pallas_call(
        logits_kernel, name="head_logits",
        grid=(num_micro, n_tile),
        out_shape=(jax.ShapeDtypeStruct((num_micro, vocab, tokens), bf), jax.ShapeDtypeStruct((num_micro, n_row, tokens), f32),
                   jax.ShapeDtypeStruct((num_micro, 8, tokens), f32), jax.ShapeDtypeStruct((num_micro, d_model, tokens), bf)),
        in_specs=[micro3((1, d_model, tokens)), micro3((1, 1, tokens)), VMEM],
        out_specs=(pl.BlockSpec((1, tile, tokens), lambda i, j: (i, j, 0)), micro3((1, n_row, tokens)), micro3((1, 8, tokens)), micro3((1, d_model, tokens))),
        scratch_shapes=[pltpu.VMEM((8, tokens), f32)],
        compiler_params=params, cost_estimate=cost(0),
    )(h_fin, lab, w_head)

    stats = lax.all_gather(stat[:, :3, :], 'pp')
    m_all, s_all = stats[:, :, 0], stats[:, :, 1]
    m_top = jnp.max(m_all, axis=0)
    s_top = jnp.sum(s_all * jnp.exp(m_all - m_top), axis=0)
    loss = jnp.sum(m_top + jnp.log(s_top) - jnp.sum(stats[:, :, 2], axis=0)) * inv
    fac = jnp.exp(m_run - m_top[:, None, :]) * (inv / s_top)[:, None, :]

    wt = jnp.swapaxes(w_head.reshape(n_tile, tile, d_model), 1, 2)
    dn = pl.pallas_call(
        functools.partial(dnorm_kernel, inv), name="head_dnorm",
        grid=(num_micro, n_tile),
        out_shape=jax.ShapeDtypeStruct((num_micro, d_model, tokens), f32),
        in_specs=[pl.BlockSpec((1, tile, tokens), lambda i, j: (i, j, 0)), micro3((1, n_row, tokens)), micro3((1, 1, tokens)), VMEM],
        out_specs=micro3((1, d_model, tokens)),
        compiler_params=params, cost_estimate=cost(0),
    )(e, fac, lab, wt)

    per = 2
    head_grad = pl.pallas_call(
        functools.partial(dhead_kernel, inv), name="head_dweight",
        grid=(n_tile, num_micro // per),
        out_shape=jax.ShapeDtypeStruct((vocab, d_model), bf),
        in_specs=[pl.BlockSpec((per, tile, tokens), lambda j, i: (i, j, 0)), pl.BlockSpec((per, n_row, tokens), lambda j, i: (i, 0, 0)),
                  pl.BlockSpec((per, 1, tokens), lambda j, i: (i, 0, 0)), pl.BlockSpec((per, d_model, tokens), lambda j, i: (i, 0, 0))],
        out_specs=pl.BlockSpec((tile, d_model), lambda j, i: (j, 0)),
        scratch_shapes=[pltpu.VMEM((tile, d_model), f32)],
        compiler_params=params, cost_estimate=cost(0),
    )(e, fac, lab, n_t)

    dn_own = lax.psum_scatter(dn, 'pp', scatter_dimension=0, tiled=True)
    per_stage = num_micro // n_stage
    h_own = lax.dynamic_slice_in_dim(h_fin, stage_id * per_stage, per_stage, 0).astype(f32)
    r_own = lax.rsqrt(jnp.mean(h_own * h_own, axis=1, keepdims=True) + NORM_EPS)
    n_own = h_own * r_own
    d_fin = r_own * (dn_own - n_own * jnp.mean(dn_own * n_own, axis=1, keepdims=True))
    return loss, head_grad, d_fin.astype(bf)


def bwd_kernel(n_stage, num_micro, dfin_ref, saved_ref, slope_ref, hid_ref, g_ref, w1_ref, w2_ref, dw1_ref, dw2_ref, dg_ref, dx_ref,
               dbuf, obuf, xbuf, h_in, slope_in, hid_in, dpre, acc1, acc2, accg, st1, st2,
               in_sem, push_sem, out_sem, x_sem, xr_sem, h_sem, slope_sem, hid_sem, w_sem):
    me = lax.axis_index("pp")
    left = lax.rem(me + n_stage - 1, n_stage)
    first, last = me == 0, me == n_stage - 1
    n_unit = 2 * num_micro
    per = num_micro // n_stage
    d_ff = w1_ref.shape[2]
    step = 512
    group_barrier(me, n_stage)

    def fetch(w):
        u, par = n_unit - 1 - w, lax.rem(w, 2)
        return (pltpu.make_async_copy(saved_ref.at[u], h_in.at[par], h_sem.at[par]),
                pltpu.make_async_copy(slope_ref.at[u], slope_in.at[par], slope_sem.at[par]),
                pltpu.make_async_copy(hid_ref.at[u], hid_in.at[par], hid_sem.at[par]))

    for copy in fetch(0):
        copy.start()

    @pl.when(last)
    def _():
        for i in range(per):
            slot = num_micro - 1 - (per * (n_stage - 1) + i)
            pltpu.make_async_copy(dfin_ref.at[i], dbuf.at[slot], in_sem.at[slot]).start()

    @pl.when(jnp.logical_not(last))
    def _():
        for i in reversed(range(per)):
            slot = num_micro - 1 - (per * me + i)
            remote(dfin_ref.at[i], dbuf.at[slot], push_sem.at[i], in_sem.at[slot], n_stage - 1).start()

    @pl.loop(0, n_unit)
    def _(w):
        half = 1 - w // num_micro
        par = lax.rem(w, 2)
        is_local = last & (w < per)
        is_final = first & (half == 0)

        @pl.when(w + 1 < n_unit)
        def _():
            for copy in fetch(w + 1):
                copy.start()

        @pl.when(lax.rem(w, num_micro) == 0)
        def _():
            acc1[...] = jnp.zeros_like(acc1)
            acc2[...] = jnp.zeros_like(acc2)
            accg[...] = jnp.zeros_like(accg)

        @pl.when(is_local)
        def _():
            pltpu.make_async_copy(dfin_ref.at[0], dbuf.at[w], in_sem.at[w]).wait()

        @pl.when(jnp.logical_not(is_local))
        def _():
            remote(obuf.at[0], dbuf.at[w], out_sem.at[0], in_sem.at[w], left).wait_recv()

        for copy in fetch(w):
            copy.wait()

        d_in = dbuf[w]
        for k in range(d_ff // step):
            rows = pl.ds(k * step, step)
            dpre[rows, :] = (nn(w2_ref[half, rows, :], d_in) * slope_in[par, rows, :]).astype(jnp.bfloat16)
        d_y = nn(w1_ref[half], dpre[...])
        h = h_in[par].astype(jnp.float32)
        r = col_scale(h)
        hr = h * r
        gain = g_ref[half]
        accg[...] += d_y * hr
        d_t = d_y * gain
        d_out = d_in.astype(jnp.float32) + r * (d_t - hr * jnp.mean(d_t * hr, axis=0, keepdims=True))

        @pl.when(is_final)
        def _():
            q = w - num_micro
            slot = lax.rem(q, 4)
            m = num_micro - 1 - q
            owner, i = m // per, lax.rem(m, per)

            @pl.when(q >= 4)
            def _():
                remote(xbuf.at[slot], dx_ref.at[0], x_sem.at[slot], xr_sem.at[0], left).wait_send()

            xbuf[slot] = d_out

            @pl.when(owner == 0)
            def _():
                pltpu.make_async_copy(xbuf.at[slot], dx_ref.at[i], x_sem.at[slot]).start()

            @pl.when(owner > 0)
            def _():
                remote(xbuf.at[slot], dx_ref.at[i], x_sem.at[slot], xr_sem.at[i], jnp.maximum(owner, 1)).start()

        @pl.when(jnp.logical_not(is_final))
        def _():
            slot = lax.rem(w, 4)

            @pl.when(w >= 4)
            def _():
                remote(obuf.at[slot], dbuf.at[w], out_sem.at[slot], in_sem.at[w], left).wait_send()

            obuf[slot] = d_out.astype(jnp.bfloat16)
            dst = w + jnp.where(first, num_micro, 0)
            remote(obuf.at[slot], dbuf.at[dst], out_sem.at[slot], in_sem.at[dst], left).start()

        y = (hr * gain).astype(jnp.bfloat16)
        for k in range(d_ff // step):
            rows = pl.ds(k * step, step)
            acc2[rows, :] += nt(hid_in[par, rows, :], d_in)
            acc1[:, rows] += nt(y, dpre[rows, :])

        @pl.when(lax.rem(w, num_micro) == num_micro - 1)
        def _():
            @pl.when(half == 0)
            def _():
                pltpu.make_async_copy(st1, dw1_ref.at[1], w_sem.at[0]).wait()
                pltpu.make_async_copy(st2, dw2_ref.at[1], w_sem.at[1]).wait()

            st1[...] = acc1[...].astype(jnp.bfloat16)
            st2[...] = acc2[...].astype(jnp.bfloat16)
            dg_ref[half] = jnp.sum(accg[...], axis=1, keepdims=True)
            pltpu.make_async_copy(st1, dw1_ref.at[half], w_sem.at[0]).start()
            pltpu.make_async_copy(st2, dw2_ref.at[half], w_sem.at[1]).start()

    pltpu.make_async_copy(st1, dw1_ref.at[0], w_sem.at[0]).wait()
    pltpu.make_async_copy(st2, dw2_ref.at[0], w_sem.at[1]).wait()
    for slot in range(4):
        remote(obuf.at[slot], dbuf.at[0], out_sem.at[slot], in_sem.at[0], left).wait_send()

    @pl.when(jnp.logical_not(last))
    def _():
        for i in range(per):
            remote(dfin_ref.at[i], dbuf.at[0], push_sem.at[i], in_sem.at[0], n_stage - 1).wait_send()

    @pl.when(first)
    def _():
        remote(xbuf.at[0], dx_ref.at[0], x_sem.at[0], xr_sem.at[0], left).wait_send()
        for slot in range(1, 4):
            pltpu.make_async_copy(xbuf.at[slot], dx_ref.at[0], x_sem.at[slot]).wait()

    @pl.when(jnp.logical_not(first))
    def _():
        for i in range(per):
            remote(xbuf.at[0], dx_ref.at[i], x_sem.at[0], xr_sem.at[i], left).wait_recv()


def run_backward(d_fin, saved, slope, hid, gains, w1, w2, n_stage):
    n_unit, d_model, tokens = saved.shape
    num_micro = n_unit // 2
    d_ff = w1.shape[2]
    per = num_micro // n_stage
    bf, f32 = jnp.bfloat16, jnp.float32
    dma = pltpu.SemaphoreType.DMA
    return pl.pallas_call(
        functools.partial(bwd_kernel, n_stage, num_micro),
        name="stack_bwd",
        out_shape=(jax.ShapeDtypeStruct(w1.shape, bf), jax.ShapeDtypeStruct(w2.shape, bf), jax.ShapeDtypeStruct((2, d_model, 1), f32),
                   jax.ShapeDtypeStruct((per, d_model, tokens), f32)),
        in_specs=[ANY, ANY, ANY, ANY, VMEM, VMEM, VMEM],
        out_specs=(ANY, ANY, VMEM, ANY),
        scratch_shapes=[
            pltpu.VMEM((n_unit, d_model, tokens), bf), pltpu.VMEM((4, d_model, tokens), bf), pltpu.VMEM((4, d_model, tokens), f32),
            pltpu.VMEM((2, d_model, tokens), bf), pltpu.VMEM((2, d_ff, tokens), f32), pltpu.VMEM((2, d_ff, tokens), bf),
            pltpu.VMEM((d_ff, tokens), bf), pltpu.VMEM((d_model, d_ff), f32), pltpu.VMEM((d_ff, d_model), f32), pltpu.VMEM((d_model, tokens), f32),
            pltpu.VMEM((d_model, d_ff), bf), pltpu.VMEM((d_ff, d_model), bf),
            dma((n_unit,)), dma((per,)), dma((4,)), dma((4,)), dma((per,)), dma((2,)), dma((2,)), dma((2,)), dma((2,)),
        ],
        compiler_params=pltpu.CompilerParams(collective_id=1, has_side_effects=True, vmem_limit_bytes=VMEM_MAX),
        cost_estimate=pl.CostEstimate(flops=8 * n_unit * tokens * d_model * d_ff, bytes_accessed=7 * n_unit * d_ff * tokens, transcendentals=0),
    )(d_fin, saved, slope, hid, gains, w1, w2)


def solution(mesh):
    n_stage = mesh.shape['pp']

    def local_step(x_embed, labels, norm_gain, w_up, w_down, w_head):
        stage_id = lax.axis_index('pp')
        gains = jnp.swapaxes(norm_gain[0], 1, 2)
        w1, w2 = w_up[0, :, 0], w_down[0, :, 0]
        saved, slope, hid, h_fin = run_forward(jnp.swapaxes(x_embed, 1, 2), gains, jnp.swapaxes(w1, 1, 2), jnp.swapaxes(w2, 1, 2), n_stage)
        loss, head_grad, d_fin = run_head(h_fin, labels, w_head, stage_id, n_stage)
        dw1, dw2, dg, dx = run_backward(d_fin, saved, slope, hid, gains, w1, w2, n_stage)
        return (loss.reshape(1), jnp.swapaxes(dx, 1, 2), jnp.swapaxes(dg, 1, 2)[None], dw1[None, :, None], dw2[None, :, None], head_grad)

    part_spec = P('dp')
    stage_spec = P('pp')
    out_spec = P(('dp', 'pp'))
    return jax.shard_map(local_step, mesh=mesh, in_specs=(part_spec, part_spec, stage_spec, stage_spec, stage_spec, stage_spec), out_specs=(part_spec, out_spec, out_spec, out_spec, out_spec, out_spec), check_vma=False)
```

time: 3280 us -> 816 us (0.25)
  matrix products: 1330 us -> 0 us
  Pallas kernels: 0 us -> 728 us
  other arithmetic: 687 us -> 10.1 us
  waiting for transfers between devices: 667 us -> 0.02 us
  local copies, waits for them, and re-layouts: 395 us -> 52.2 us
  blocking collectives: 138 us -> 8.63 us
    dot_general x198 -> x0, matrix products: 1330 us -> none  [the longest x66 598 us: contract_first(): lax.dot_general(lhs_mat, rhs_mat, (((0,), (0,)), ((), ())), preferred_ele...]
    pallas_call x0 -> x5, Pallas kernels: none -> 728 us  [the longest x1 191 us: run_backward(): pl.pallas_call(functools.partial(bwd_kernel, n_stage, num_micro), name='s...]
    psum x24 -> x0, waiting for transfers between devices: 368 us -> none  [the longest x12 318 us: head_step(): h_norm = lax.psum(jnp.where(is_last, h_norm, jnp.zeros_like(h_norm)), 'pp')]
    dynamic_slice x186 -> x0, local copies, waits for them, and re-layouts: 289 us -> none  [take_row(): return lax.dynamic_index_in_dim(buffer, row_id, 0, False)]
    ppermute x54 -> x0, waiting for transfers between devices: 232 us -> none  [the longest x27 232 us: fwd_step(): act_carry = lax.ppermute(h_cur, 'pp', to_next)]
    convert_element_type x40 -> x1, other arithmetic: 229 us -> 3.27 us  [run_head(): return (loss, head_grad, d_fin.astype(bf))]
    reduce_sum x102 -> x3, other arithmetic: 226 us -> 4.8 us  [the longest x1 3.03 us: run_head(): jnp.mean(dn_own * n_own, axis=1, keepdims=True)]
    dynamic_update_slice x93 -> x0, other arithmetic: 156 us -> none  [the longest x66 156 us: masked_store(): lax.dynamic_update_index_in_dim(buffer, jnp.where(keep_mask, new_value, p...]
  transfers between devices with their start and end apart: 79 -> 1, of which waited for: 52 -> 0; matrix products, arithmetic and copies ran while one was open for 29% -> 0% of each run, Pallas kernels for 0% -> 12%
where the time goes in v1:
time: 816 us; the launch traced here: 815 us
  Pallas kernels  728 us (89%)
  local copies, waits for them, and re-layouts  52.2 us (6%)
  between operations  15.9 us (2%)
  other arithmetic  10.1 us (1%)
  blocking collectives  8.63 us (1%)
    pallas_call x1, Pallas kernels, run_backward(): pl.pallas_call(functools.partial(bwd_kernel, n_stage, num_micro), name='s...  191 us
    pallas_call x1, Pallas kernels, run_forward(): pl.pallas_call(functools.partial(fwd_kernel, n_stage, num_micro), name='s...  175 us
    pallas_call x1, Pallas kernels, run_head(): pl.pallas_call(logits_kernel, name='head_logits', grid=(num_micro, n_tile...  164 us
    pallas_call x1, Pallas kernels, run_head(): pl.pallas_call(functools.partial(dnorm_kernel, inv), name='head_dnorm', g...  104 us
    pallas_call x1, Pallas kernels, run_head(): pl.pallas_call(functools.partial(dhead_kernel, inv), name='head_dweight',...  94.1 us
    unnamed x16, local copies, waits for them, and re-layouts  19.5 us
    reshape x1, local copies, waits for them, and re-layouts, run_head(): wt = jnp.swapaxes(w_head.reshape(n_tile, tile, d_model), 1, 2)  17.2 us
  transfers between devices with their start and end apart: 1, of which 0 were waited for; matrix products, arithmetic and copies ran while one was open for 0% of the time, Pallas kernels for 12%

profile of v1, /device:TPU:0, one launch (start us, length us, event | category | flops | bytes accessed | tf_op | source)
XLA Modules:
  0.0 815.1 jit_solution(939480566432296442)
XLA Ops:
  7.2 0.0 reduce-scatter.4.cloned.1.call-start
  7.2 8.6 %copy.42 = bf16[12,512,512]{1,2,0:T(8,128)(2,1)} copy(bf16[12,512,512]{2,1,0:T(8,128)(2,1)} %param.6) | data formatting | bytes 12582912 | tf_op args[0]
  15.8 0.0 copy-done.5
  15.9 1.0 transpose_squeeze.4.g_ref
  16.9 6.2 copy.44.w1t_ref
  23.1 6.2 copy.45.w2t_ref
  29.3 0.6 reshape.38.lab_ref
  29.9 175.3 %stack_fwd.1 = (bf16[24,512,512]{2,1,0:T(8,128)(2,1)}, f32[24,2048,512]{2,1,0:T(8,128)}, bf16[24,2048,512]{2,1,0:T(8,128)(2,1)}, bf16[12,512,512]{2,1,0:T(8,128)(2,1)}) custom-call(bf16[12,512,512]{2,1,0:T(8,128)(2,1)} %bitcast.35, f32[2,512,1]{2,1,0:T(8,128)} %transpose_squeeze.4.g_ref, bf16[2,2048,512]{2,1,0:T(8,128)(2,1)} %copy.44.w1t_ref, ...), custom_call_target="tpu_custom_call" | custom-call | flops 51539607552 | bytes 176160768 | tf_op jit(solution)/shard_map/stack_fwd/pallas_call | solution.py:161
  205.2 164.1 %head_logits.1 = (bf16[12,12576,512]{2,1,0:T(8,128)(2,1)}, f32[12,16,512]{2,1,0:T(8,128)}, f32[12,8,512]{2,1,0:T(8,128)}, bf16[12,512,512]{2,1,0:T(8,128)(2,1)}) custom-call(bf16[12,512,512]{2,1,0:T(8,128)(2,1)} %get-tuple-element.18.h_ref, s32[12,1,512]{2,1,0:T(1,128)} %reshape.38.lab_ref, bf16[12576,512]{1,0:T(8,128)(2,1)} %w_ref.1), custom_call_target="tpu_custom_call" | custom-call | flops 79121350656 | bytes 154533888 | tf_op jit(solution)/shard_map/head_logits/pallas_call | solution.py:279
  369.3 0.9 slice.12
  370.3 8.6 %all-gather = f32[48,3,512]{2,1,0:T(4,128)S(1)} all-gather(f32[12,3,512]{2,1,0:T(4,128)S(1)} %slice.12), channel_id=2, replica_groups=mesh['dp'=2,'pp'=4] {'pp'}, dimensions={0}, use_global_device_ids=true | all-gather | bytes 368640 | tf_op jit(solution)/shard_map/all_gather | solution.py:290
  378.9 0.3 fusion.11
  379.3 0.0 copy-start.3
  379.3 17.2 %copy.49 = bf16[3,4192,512]{1,2,0:T(8,128)(2,1)} copy(bf16[3,4192,512]{2,1,0:T(8,128)(2,1)} %bitcast.34) | data formatting | bytes 25755648 | tf_op jit(solution)/shard_map/reshape | solution.py:297
  396.5 0.6 broadcast_divide_fusion
  397.1 0.0 copy-done.3
  397.1 0.8 exponential_multiply_fusion.fac_ref
  397.9 103.8 %head_dnorm.1 = f32[12,512,512]{2,1,0:T(8,128)} custom-call(bf16[12,12576,512]{2,1,0:T(8,128)(2,1)} %get-tuple-element.20.e_ref, f32[12,16,512]{2,1,0:T(8,128)} %exponential_multiply_fusion.fac_ref, s32[12,1,512]{2,1,0:T(1,128)} %reshape.38.lab_ref, bf16[3,512,4192]{2,1,0:T(8,128)(2,1)} %bitcast.33), custom_call_target="tpu_custom_call" | custom-call | flops 79121350656 | bytes 154533888 | tf_op jit(solution)/shard_map/head_dnorm/pallas_call | solution.py:298
  501.8 0.0 reduce-scatter.4.cloned.1.call-update
  502.5 1.7 fusion.6
  504.2 94.1 %head_dweight.1 = bf16[12576,512]{1,0:T(8,128)(2,1)} custom-call(bf16[12,12576,512]{2,1,0:T(8,128)(2,1)} %get-tuple-element.20.e_ref, f32[12,16,512]{2,1,0:T(8,128)} %exponential_multiply_fusion.fac_ref, s32[12,1,512]{2,1,0:T(1,128)} %reshape.38.lab_ref, bf16[12,512,512]{2,1,0:T(8,128)(2,1)} %get-tuple-element.29.n_ref), custom_call_target="tpu_custom_call" | custom-call | flops 79121350656 | bytes 154533888 | tf_op jit(solution)/shard_map/head_dweight/pallas_call | solution.py:308
  598.3 3.0 fusion.2
  601.3 0.3 copy-done
  601.6 3.3 fusion.5.dfin_ref
  604.9 190.8 %stack_bwd.1 = (bf16[2,512,2048]{2,1,0:T(8,128)(2,1)}, bf16[2,2048,512]{2,1,0:T(8,128)(2,1)}, f32[2,512,1]{2,1,0:T(8,128)}, f32[3,512,512]{2,1,0:T(8,128)}) custom-call(bf16[3,512,512]{2,1,0:T(8,128)(2,1)} %fusion.5.dfin_ref, bf16[24,512,512]{2,1,0:T(8,128)(2,1)} %get-tuple-element.22.saved_ref, f32[24,2048,512]{2,1,0:T(8,128)} %get-tuple-element.23.slope_ref, ...), custom_call_target="tpu_custom_call" | custom-call | flops 103079215104 | bytes 176160768 | tf_op jit(solution)/shard_map/stack_bwd/pallas_call | solution.py:484
  795.7 0.0 copy-start.2
  795.7 3.6 copy.51
  799.3 0.2 reduce.3
  799.5 0.6 broadcast_in_dim_transpose.4
  800.1 4.9 copy.76
  805.1 0.0 copy-done.1
  805.1 2.0 copy.77
  (12 shorter events, 0.1 us)
Async XLA Ops:
  7.2 591.1 %reduce-scatter.4.cloned.1.call-start = ((), (), s32[]{:S(2)}) async-start(), calls=%async_computation.1 | async-start | bytes 15728640
  7.2 8.6 %copy-start.5 = (f32[1,2,1,512]{3,2,1,0:T(1,128)S(1)}, f32[1,2,1,512]{3,2,1,0:T(1,128)}, u32[]{:S(2)}) copy-start(f32[1,2,1,512]{3,2,1,0:T(1,128)} %param.8) | copy-start | bytes 12292
  23.1 6.2 copy-start.4
  379.3 17.9 %copy-start.3 = (f32[12,16,512]{2,1,0:T(8,128)S(1)}, f32[12,16,512]{2,1,0:T(8,128)}, u32[]{:S(2)}) copy-start(f32[12,16,512]{2,1,0:T(8,128)} %get-tuple-element.21) | copy-start | bytes 1179652
  598.3 3.3 copy-start
  795.7 3.6 copy-start.2
  800.1 4.9 copy-start.1
Sparse Core Ops, SparseCore 0:
  501.9 91.6 reduce-scatter.3

commit v2 on v1

--- a/solution.py
+++ b/solution.py
@@ -48,14 +48,29 @@
     return pltpu.make_async_remote_copy(src_ref=src, dst_ref=dst, send_sem=send_sem, recv_sem=recv_sem, device_id={"pp": dev}, device_id_type=pl.DeviceIdType.MESH)
 
 
-def fwd_kernel(n_stage, num_micro, x_ref, g_ref, w1t_ref, w2t_ref, saved_ref, slope_ref, hid_ref, hfin_ref,
-               hbuf, obuf, fbuf, slope_st, hid_st, in_sem, out_sem, save_sem, slope_sem, hid_sem, fin_sem, fin_a, fin_b, fin_c):
+def fwd_kernel(n_stage, num_micro, x_ref, g_ref, w1_ref, w2_ref, wh_ref, saved_ref, slope_ref, hid_ref, hfin_ref, n_ref, wht_ref,
+               w1t, w2t, hbuf, obuf, fbuf, slope_st, hid_st, wh_in, wh_out, wh_last, wht_last, in_sem, out_sem, save_sem, slope_sem, hid_sem, fin_sem, fin_a, fin_b, fin_c, whi_sem, who_sem):
     me = lax.axis_index("pp")
     right = lax.rem(me + 1, n_stage)
     first, last = me == 0, me == n_stage - 1
     n_unit = 2 * num_micro
-    d_ff = w1t_ref.shape[1]
+    d_ff = w1_ref.shape[2]
+    n_tile, tile = wht_ref.shape[0], wht_ref.shape[2]
+    subs = sub_tiles(tile)
     group_barrier(me, n_stage)
+
+    def emit_norm(m):
+        hf = fbuf[m].astype(jnp.float32)
+        hbuf[m] = (hf * col_scale(hf)).astype(jnp.bfloat16)
+        pltpu.make_async_copy(hbuf.at[m], n_ref.at[m], save_sem.at[m]).start()
+
+    def head_copies(t, k):
+        off, size = subs[k]
+        last_sub = k + 1 == len(subs)
+        src, dst = (wh_last, wht_last) if last_sub else (wh_in, wh_out)
+        rows = pl.ds(pl.multiple_of(t * tile + off, 16), size)
+        return (src, dst, pltpu.make_async_copy(wh_ref.at[rows, :], src, whi_sem.at[int(last_sub)]),
+                pltpu.make_async_copy(dst, wht_ref.at[t, :, off:off + size], who_sem.at[int(last_sub)]))
 
     @pl.when(first)
     def _():
@@ -66,6 +81,12 @@
     @pl.loop(0, n_unit)
     def _(u):
         half = u // num_micro
+
+        @pl.when(lax.rem(u, num_micro) == 0)
+        def _():
+            w1t[...] = w1_ref[half].T
+            w2t[...] = w2_ref[half].T
+
         m = lax.rem(u, num_micro)
         from_x = first & (half == 0)
         is_final = last & (half == 1)
@@ -74,6 +95,7 @@
         @pl.when(from_x)
         def _():
             pltpu.make_async_copy(x_ref.at[m], hbuf.at[u], in_sem.at[u]).wait()
+            hbuf[u] = hbuf[u].T
 
         @pl.when(jnp.logical_not(from_x))
         def _():
@@ -89,12 +111,16 @@
         h = hbuf[u].astype(jnp.float32)
         y = (h * col_scale(h) * g_ref[half]).astype(jnp.bfloat16)
         step = 512
+        pre = nn(w1t[0:step, :], y)
         for k in range(d_ff // step):
             rows = pl.ds(k * step, step)
-            hid, slope = gelu_pair(nn(w1t_ref[half, rows, :], y))
+            cur = pre
+            if k + 1 < d_ff // step:
+                pre = nn(w1t[(k + 1) * step:(k + 2) * step, :], y)
+            hid, slope = gelu_pair(cur)
             hid_st[par, rows, :] = hid.astype(jnp.bfloat16)
             slope_st[par, rows, :] = slope
-        out = (h + nn(w2t_ref[half], hid_st[par])).astype(jnp.bfloat16)
+        out = (h + nn(w2t[...], hid_st[par])).astype(jnp.bfloat16)
         pltpu.make_async_copy(slope_st.at[par], slope_ref.at[u], slope_sem.at[par]).start()
         pltpu.make_async_copy(hid_st.at[par], hid_ref.at[u], hid_sem.at[par]).start()
 
@@ -102,8 +128,10 @@
         def _():
             fbuf[m] = out
             pltpu.make_async_copy(fbuf.at[m], hfin_ref.at[m], fin_c.at[m]).start()
-            remote(fbuf.at[m], hfin_ref.at[m], fin_a.at[m], fin_sem.at[m], n_stage - 2).start()
-            remote(fbuf.at[m], hfin_ref.at[m], fin_b.at[m], fin_sem.at[m], 1).start()
+            remote(fbuf.at[m], fbuf.at[m], fin_a.at[m], fin_sem.at[m], n_stage - 2).start()
+            remote(fbuf.at[m], fbuf.at[m], fin_b.at[m], fin_sem.at[m], 1).start()
+            pltpu.make_async_copy(hbuf.at[m], saved_ref.at[m], save_sem.at[m]).wait()
+            emit_norm(m)
 
         @pl.when(jnp.logical_not(is_final))
         def _():
@@ -116,6 +144,20 @@
             obuf[slot] = out
             dst = u + jnp.where(last, num_micro, 0)
             remote(obuf.at[slot], hbuf.at[dst], out_sem.at[slot], in_sem.at[dst], right).start()
+
+        for k in range(len(subs)):
+            @pl.when((lax.rem(u, 2 * len(subs)) == 2 * k) & (u // (2 * len(subs)) < n_tile))
+            def _(k=k):
+                head_copies(u // (2 * len(subs)), k)[2].start()
+
+            @pl.when((lax.rem(u, 2 * len(subs)) == 2 * k + 1) & (u // (2 * len(subs)) < n_tile))
+            def _(k=k):
+                t = u // (2 * len(subs))
+                src, dst, copy_in, copy_out = head_copies(t, k)
+                copy_in.wait()
+                dst[...] = src[...].T
+                copy_out.start()
+                copy_out.wait()
 
     for slot in range(4):
         remote(obuf.at[slot], hbuf.at[0], out_sem.at[slot], in_sem.at[0], right).wait_send()
@@ -132,47 +174,61 @@
         @pl.loop(0, num_micro)
         def _(m):
             pltpu.make_async_copy(fbuf.at[m], hfin_ref.at[m], fin_c.at[m]).wait()
-            remote(fbuf.at[m], hfin_ref.at[m], fin_a.at[m], fin_sem.at[m], n_stage - 2).wait_send()
-            remote(fbuf.at[m], hfin_ref.at[m], fin_b.at[m], fin_sem.at[m], 1).wait_send()
+            remote(fbuf.at[m], fbuf.at[m], fin_a.at[m], fin_sem.at[m], n_stage - 2).wait_send()
+            remote(fbuf.at[m], fbuf.at[m], fin_b.at[m], fin_sem.at[m], 1).wait_send()
 
     @pl.when(jnp.logical_not(last))
     def _():
         @pl.loop(0, num_micro)
         def _(m):
-            remote(fbuf.at[m], hfin_ref.at[m], fin_a.at[m], fin_sem.at[m], right).wait_recv()
+            remote(fbuf.at[m], fbuf.at[m], fin_a.at[m], fin_sem.at[m], right).wait_recv()
 
             @pl.when(me == 1)
             def _():
-                remote(hfin_ref.at[m], hfin_ref.at[m], fin_a.at[m], fin_sem.at[m], 0).start()
-
-    @pl.when(me == 1)
-    def _():
+                remote(fbuf.at[m], fbuf.at[m], fin_a.at[m], fin_sem.at[m], 0).start()
+
+            pltpu.make_async_copy(fbuf.at[m], hfin_ref.at[m], fin_c.at[m]).start()
+            emit_norm(m)
+
         @pl.loop(0, num_micro)
         def _(m):
-            remote(hfin_ref.at[m], hfin_ref.at[m], fin_a.at[m], fin_sem.at[m], 0).wait_send()
-
-
-def run_forward(x_t, gains, w1t, w2t, n_stage):
-    num_micro, d_model, tokens = x_t.shape
-    d_ff = w1t.shape[1]
+            pltpu.make_async_copy(fbuf.at[m], hfin_ref.at[m], fin_c.at[m]).wait()
+            pltpu.make_async_copy(hbuf.at[m], n_ref.at[m], save_sem.at[m]).wait()
+
+    @pl.when(me == 1)
+    def _():
+        @pl.loop(0, num_micro)
+        def _(m):
+            remote(fbuf.at[m], fbuf.at[m], fin_a.at[m], fin_sem.at[m], 0).wait_send()
+
+
+def run_forward(x_embed, gains, w1, w2, w_head, n_tile, n_stage):
+    num_micro, tokens, d_model = x_embed.shape
+    d_ff = w1.shape[2]
     bf, f32 = jnp.bfloat16, jnp.float32
     n_unit = 2 * num_micro
+    tile = w_head.shape[0] // n_tile
+    last_rows = sub_tiles(tile)[-1][1]
     dma = pltpu.SemaphoreType.DMA
     return pl.pallas_call(
         functools.partial(fwd_kernel, n_stage, num_micro),
         name="stack_fwd",
         out_shape=(jax.ShapeDtypeStruct((n_unit, d_model, tokens), bf), jax.ShapeDtypeStruct((n_unit, d_ff, tokens), f32),
-                   jax.ShapeDtypeStruct((n_unit, d_ff, tokens), bf), jax.ShapeDtypeStruct((num_micro, d_model, tokens), bf)),
-        in_specs=[ANY, VMEM, VMEM, VMEM],
-        out_specs=(ANY, ANY, ANY, ANY),
+                   jax.ShapeDtypeStruct((n_unit, d_ff, tokens), bf), jax.ShapeDtypeStruct((num_micro, d_model, tokens), bf),
+                   jax.ShapeDtypeStruct((num_micro, d_model, tokens), bf), jax.ShapeDtypeStruct((n_tile, d_model, tile), bf)),
+        in_specs=[ANY, VMEM, VMEM, VMEM, ANY],
+        out_specs=(ANY, ANY, ANY, ANY, ANY, ANY),
         scratch_shapes=[
+            pltpu.VMEM((d_ff, d_model), bf), pltpu.VMEM((d_model, d_ff), bf),
             pltpu.VMEM((n_unit, d_model, tokens), bf), pltpu.VMEM((4, d_model, tokens), bf), pltpu.VMEM((num_micro, d_model, tokens), bf),
             pltpu.VMEM((2, d_ff, tokens), f32), pltpu.VMEM((2, d_ff, tokens), bf),
+            pltpu.VMEM((SUB, d_model), bf), pltpu.VMEM((d_model, SUB), bf), pltpu.VMEM((last_rows, d_model), bf), pltpu.VMEM((d_model, last_rows), bf),
             dma((n_unit,)), dma((4,)), dma((n_unit,)), dma((2,)), dma((2,)), dma((num_micro,)), dma((num_micro,)), dma((num_micro,)), dma((num_micro,)),
+            dma((2,)), dma((2,)),
         ],
         compiler_params=pltpu.CompilerParams(collective_id=0, has_side_effects=True, vmem_limit_bytes=VMEM_MAX),
         cost_estimate=pl.CostEstimate(flops=4 * n_unit * tokens * d_model * d_ff, bytes_accessed=7 * n_unit * d_ff * tokens, transcendentals=0),
-    )(x_t, gains, w1t, w2t)
+    )(x_embed, gains, w1, w2, w_head)
 
 
 def sub_tiles(tile):
@@ -180,35 +236,96 @@
     return [(k * SUB, SUB if k + 1 < n_sub else tile - k * SUB) for k in range(n_sub)]
 
 
-def logits_kernel(h_ref, lab_ref, w_ref, e_ref, mrun_ref, stat_ref, n_ref, run):
-    j = pl.program_id(1)
-    tile = e_ref.shape[1]
+def label_group(lab):
+    return jnp.where(lax.broadcasted_iota(jnp.int32, (8, lab.shape[1]), 0) == (lab & 7), lab >> 3, -1)
+
+
+def logits_kernel(tile, n_all, lab_ref, w_ref, e_ref, mrun_ref, stat_ref, z0, z1, run):
+    i = pl.program_id(0)
+    num_micro = pl.num_programs(0)
+    vocab, tokens = e_ref.shape[1], e_ref.shape[2]
     subs = sub_tiles(tile)
-
-    @pl.when(j == 0)
-    def _():
-        run[0:1, :] = jnp.full((1, run.shape[1]), -jnp.inf, jnp.float32)
-        run[1:3, :] = jnp.zeros((2, run.shape[1]), jnp.float32)
-        h = h_ref[0].astype(jnp.float32)
-        n_ref[0] = (h * col_scale(h)).astype(jnp.bfloat16)
-
-    n = n_ref[0]
-    lab = lab_ref[0] - j * tile
-    m_run, s_run, z_lab = run[0:1, :], run[1:2, :], run[2:3, :]
-    for k, (off, size) in enumerate(subs):
-        z = nn(w_ref[pl.ds(pl.multiple_of(j * tile + off, 16), size), :], n)
-        m_new = jnp.maximum(m_run, jnp.max(z, axis=0, keepdims=True))
-        e = jnp.exp(z - m_new)
-        e_ref[0, off:off + size, :] = e.astype(jnp.bfloat16)
-        s_run = s_run * jnp.exp(m_run - m_new) + jnp.sum(e, axis=0, keepdims=True)
-        hit = lax.broadcasted_iota(jnp.int32, z.shape, 0) == lab - off
-        z_lab = z_lab + jnp.sum(jnp.where(hit, z, 0.0), axis=0, keepdims=True)
-        m_run = m_new
-        mrun_ref[0, pl.ds(j * len(subs) + k, 1), :] = m_run
-    run[0:1, :] = m_run
-    run[1:2, :] = s_run
-    run[2:3, :] = z_lab
-    stat_ref[0] = run[...]
+    n_sub, n_tile = len(subs), vocab // tile
+    zbuf = (z0, z1)
+    piece = 256
+    low = jnp.full((8, tokens), -jnp.inf, jnp.float32)
+
+    def rows_at(t, off, size):
+        return pl.ds(pl.multiple_of(t * tile + off, 16), size)
+
+    def dot_part(dst, t, off, size, base, n, group, top, hit):
+        z = nn(w_ref[rows_at(t, off, size), :], n)
+        dst[off - base:off - base + size, :] = z
+        for g in range(size // 8):
+            zg = z[g * 8:g * 8 + 8, :]
+            top = jnp.maximum(top, zg)
+            hit = jnp.where(group == t * (tile // 8) + (off // 8 + g), zg, hit)
+        return top, hit
+
+    def exp_part(src, t, base, lo, hi, m16, s8):
+        for r in range(lo, hi, 16):
+            e = jnp.exp(src[r:r + 16, :] - m16)
+            e_ref[0, rows_at(t, base + r, 16), :] = e.astype(jnp.bfloat16)
+            s8 = s8 + (e[0:8, :] + e[8:16, :])
+        return s8
+
+    def pieces(size):
+        n_piece = size // piece
+        return [(q * piece, piece if q + 1 < n_piece else size - q * piece) for q in range(n_piece)]
+
+    def first_dot(m):
+        n, group, top, hit = n_all[m], label_group(lab_ref[m]), low, jnp.zeros((8, tokens), jnp.float32)
+        return n, group, top, hit
+
+    def joint(kn, tn, n, group, top, hit, kc, tc, m, s8):
+        m16 = jnp.broadcast_to(m, (16, tokens))
+        base_n, size_n = subs[kn]
+        base_c, size_c = subs[kc]
+        parts = pieces(size_n)
+        cut = -(-size_c // (16 * len(parts))) * 16
+        for q, (off, size) in enumerate(parts):
+            top, hit = dot_part(zbuf[kn % 2], tn, base_n + off, size, base_n, n, group, top, hit)
+            s8 = exp_part(zbuf[kc % 2], tc, base_c, min(q * cut, size_c), min((q + 1) * cut, size_c), m16, s8)
+        return top, hit, s8
+
+    @pl.when(i == 0)
+    def _():
+        n, group, top, hit = first_dot(0)
+        for off, size in pieces(subs[0][1]):
+            top, hit = dot_part(z0, 0, off, size, 0, n, group, top, hit)
+        run[0:8, :] = top
+        run[8:16, :] = hit
+
+    n = n_all[i]
+    group = label_group(lab_ref[i])
+
+    def step(kn, tn, kc, tc, carry):
+        m, s8, hit = carry
+        top, hit, s8 = joint(kn, tn, n, group, low, hit, kc, tc, m, s8)
+        m_new = jnp.maximum(m, jnp.max(top, axis=0, keepdims=True))
+        mrun_ref[0, pl.ds(tn * n_sub + kn, 1), :] = m_new
+        return m_new, s8 * jnp.exp(m - m_new), hit
+
+    m = jnp.max(run[0:8, :], axis=0, keepdims=True)
+    mrun_ref[0, 0:1, :] = m
+    carry = (m, jnp.zeros((8, tokens), jnp.float32), run[8:16, :])
+
+    def body(t, carry):
+        for k in range(n_sub):
+            carry = step((k + 1) % n_sub, t + (k + 1) // n_sub, k, t, carry)
+        return carry
+
+    carry = lax.fori_loop(0, n_tile - 1, body, carry)
+    for k in range(n_sub - 1):
+        carry = step(k + 1, n_tile - 1, k, n_tile - 1, carry)
+    m, s8, hit = carry
+    n2, group2, top2, hit2 = first_dot(jnp.minimum(i + 1, num_micro - 1))
+    top2, hit2, s8 = joint(0, 0, n2, group2, top2, hit2, n_sub - 1, n_tile - 1, m, s8)
+    run[0:8, :] = top2
+    run[8:16, :] = hit2
+    stat_ref[0, 0:1, :] = m
+    stat_ref[0, 1:2, :] = jnp.sum(s8, axis=0, keepdims=True)
+    stat_ref[0, 2:3, :] = jnp.sum(hit, axis=0, keepdims=True)
 
 
 def d_logits(e_tile, fac_row, lab, off, inv):
@@ -259,33 +376,34 @@
         out_ref[...] = acc[...].astype(jnp.bfloat16)
 
 
-def run_head(h_fin, labels, w_head, stage_id, n_stage):
+def run_head(h_fin, n_t, wt, labels, w_head, stage_id, n_stage):
     num_micro, d_model, tokens = h_fin.shape
     vocab = w_head.shape[0]
-    n_tile = 3
-    tile = vocab // n_tile
+    n_tile, tile = wt.shape[0], wt.shape[2]
     n_row = 16
     bf, f32 = jnp.bfloat16, jnp.float32
     inv = 1.0 / (num_micro * tokens)
     lab = (labels - stage_id * vocab).reshape(num_micro, 1, tokens)
     params = pltpu.CompilerParams(vmem_limit_bytes=VMEM_MAX)
-    flops = 2 * num_micro * tokens * d_model * vocab
-    e_bytes = 2 * num_micro * tokens * vocab
-
-    def cost(extra):
-        return pl.CostEstimate(flops=flops, bytes_accessed=e_bytes + extra, transcendentals=0)
-
-    micro3 = lambda shape: pl.BlockSpec(shape, lambda i, j: (i, 0, 0))
-    e, m_run, stat, n_t = pl.pallas_call(
-        logits_kernel, name="head_logits",
-        grid=(num_micro, n_tile),
+    cost = pl.CostEstimate(flops=2 * num_micro * tokens * d_model * vocab, bytes_accessed=2 * num_micro * tokens * vocab, transcendentals=0)
+
+    def micro(shape):
+        return pl.BlockSpec(shape, lambda i: (i, 0, 0))
+
+    def micro2(shape):
+        return pl.BlockSpec(shape, lambda i, j: (i, 0, 0))
+
+    z_rows = tile - (tile // SUB - 1) * SUB
+    e, m_run, stat = pl.pallas_call(
+        functools.partial(logits_kernel, tile), name="head_logits",
+        grid=(num_micro,),
         out_shape=(jax.ShapeDtypeStruct((num_micro, vocab, tokens), bf), jax.ShapeDtypeStruct((num_micro, n_row, tokens), f32),
-                   jax.ShapeDtypeStruct((num_micro, 8, tokens), f32), jax.ShapeDtypeStruct((num_micro, d_model, tokens), bf)),
-        in_specs=[micro3((1, d_model, tokens)), micro3((1, 1, tokens)), VMEM],
-        out_specs=(pl.BlockSpec((1, tile, tokens), lambda i, j: (i, j, 0)), micro3((1, n_row, tokens)), micro3((1, 8, tokens)), micro3((1, d_model, tokens))),
-        scratch_shapes=[pltpu.VMEM((8, tokens), f32)],
-        compiler_params=params, cost_estimate=cost(0),
-    )(h_fin, lab, w_head)
+                   jax.ShapeDtypeStruct((num_micro, 8, tokens), f32)),
+        in_specs=[VMEM, VMEM, VMEM],
+        out_specs=(micro((1, vocab, tokens)), micro((1, n_row, tokens)), micro((1, 8, tokens))),
+        scratch_shapes=[pltpu.VMEM((z_rows, tokens), f32), pltpu.VMEM((z_rows, tokens), f32), pltpu.VMEM((16, tokens), f32)],
+        compiler_params=params, cost_estimate=cost,
+    )(n_t, lab, w_head)
 
     stats = lax.all_gather(stat[:, :3, :], 'pp')
     m_all, s_all = stats[:, :, 0], stats[:, :, 1]
@@ -294,14 +412,13 @@
     loss = jnp.sum(m_top + jnp.log(s_top) - jnp.sum(stats[:, :, 2], axis=0)) * inv
     fac = jnp.exp(m_run - m_top[:, None, :]) * (inv / s_top)[:, None, :]
 
-    wt = jnp.swapaxes(w_head.reshape(n_tile, tile, d_model), 1, 2)
     dn = pl.pallas_call(
         functools.partial(dnorm_kernel, inv), name="head_dnorm",
         grid=(num_micro, n_tile),
         out_shape=jax.ShapeDtypeStruct((num_micro, d_model, tokens), f32),
-        in_specs=[pl.BlockSpec((1, tile, tokens), lambda i, j: (i, j, 0)), micro3((1, n_row, tokens)), micro3((1, 1, tokens)), VMEM],
-        out_specs=micro3((1, d_model, tokens)),
-        compiler_params=params, cost_estimate=cost(0),
+        in_specs=[pl.BlockSpec((1, tile, tokens), lambda i, j: (i, j, 0)), micro2((1, n_row, tokens)), micro2((1, 1, tokens)), VMEM],
+        out_specs=micro2((1, d_model, tokens)),
+        compiler_params=params, cost_estimate=cost,
     )(e, fac, lab, wt)
 
     per = 2
@@ -313,7 +430,7 @@
                   pl.BlockSpec((per, 1, tokens), lambda j, i: (i, 0, 0)), pl.BlockSpec((per, d_model, tokens), lambda j, i: (i, 0, 0))],
         out_specs=pl.BlockSpec((tile, d_model), lambda j, i: (j, 0)),
         scratch_shapes=[pltpu.VMEM((tile, d_model), f32)],
-        compiler_params=params, cost_estimate=cost(0),
+        compiler_params=params, cost_estimate=cost,
     )(e, fac, lab, n_t)
 
     dn_own = lax.psum_scatter(dn, 'pp', scatter_dimension=0, tiled=True)
@@ -326,14 +443,14 @@
 
 
 def bwd_kernel(n_stage, num_micro, dfin_ref, saved_ref, slope_ref, hid_ref, g_ref, w1_ref, w2_ref, dw1_ref, dw2_ref, dg_ref, dx_ref,
-               dbuf, obuf, xbuf, h_in, slope_in, hid_in, dpre, acc1, acc2, accg, st1, st2,
+               dbuf, obuf, xbuf, h_in, slope_in, hid_in, dpre, acc1, acc2, accg, st1, st2, gb, hrb, dyb, yb,
                in_sem, push_sem, out_sem, x_sem, xr_sem, h_sem, slope_sem, hid_sem, w_sem):
     me = lax.axis_index("pp")
     left = lax.rem(me + n_stage - 1, n_stage)
     first, last = me == 0, me == n_stage - 1
     n_unit = 2 * num_micro
     per = num_micro // n_stage
-    d_ff = w1_ref.shape[2]
+    d_model, d_ff = w1_ref.shape[1:]
     step = 512
     group_barrier(me, n_stage)
 
@@ -375,6 +492,7 @@
             acc1[...] = jnp.zeros_like(acc1)
             acc2[...] = jnp.zeros_like(acc2)
             accg[...] = jnp.zeros_like(accg)
+            gb[...] = jnp.broadcast_to(g_ref[half], gb.shape)
 
         @pl.when(is_local)
         def _():
@@ -388,17 +506,29 @@
             copy.wait()
 
         d_in = dbuf[w]
+        nxt = nn(w2_ref[half, 0:step, :], d_in)
         for k in range(d_ff // step):
             rows = pl.ds(k * step, step)
-            dpre[rows, :] = (nn(w2_ref[half, rows, :], d_in) * slope_in[par, rows, :]).astype(jnp.bfloat16)
-        d_y = nn(w1_ref[half], dpre[...])
+            cur = nxt
+            if k + 1 < d_ff // step:
+                nxt = nn(w2_ref[half, (k + 1) * step:(k + 2) * step, :], d_in)
+            dpre[rows, :] = (cur * slope_in[par, rows, :]).astype(jnp.bfloat16)
         h = h_in[par].astype(jnp.float32)
         r = col_scale(h)
-        hr = h * r
-        gain = g_ref[half]
-        accg[...] += d_y * hr
-        d_t = d_y * gain
-        d_out = d_in.astype(jnp.float32) + r * (d_t - hr * jnp.mean(d_t * hr, axis=0, keepdims=True))
+        r16 = jnp.broadcast_to(r, (16, r.shape[1]))
+        for q in range(0, d_model, 16):
+            hr = h_in[par, q:q + 16, :].astype(jnp.float32) * r16
+            hrb[q:q + 16, :] = hr
+            yb[q:q + 16, :] = (hr * gb[q:q + 16, :]).astype(jnp.bfloat16)
+        dyb[...] = nn(w1_ref[half], dpre[...])
+        dots = jnp.zeros_like(r16)
+        for q in range(0, d_model, 16):
+            prod = dyb[q:q + 16, :] * hrb[q:q + 16, :]
+            accg[q:q + 16, :] += prod
+            dots = dots + prod * gb[q:q + 16, :]
+        mean16 = jnp.broadcast_to(jnp.sum(dots, axis=0, keepdims=True) * (1.0 / d_model), r16.shape)
+        for q in range(0, d_model, 16):
+            dyb[q:q + 16, :] = dbuf[w, q:q + 16, :].astype(jnp.float32) + r16 * (dyb[q:q + 16, :] * gb[q:q + 16, :] - hrb[q:q + 16, :] * mean16)
 
         @pl.when(is_final)
         def _():
@@ -411,7 +541,7 @@
             def _():
                 remote(xbuf.at[slot], dx_ref.at[0], x_sem.at[slot], xr_sem.at[0], left).wait_send()
 
-            xbuf[slot] = d_out
+            xbuf[slot] = dyb[...]
 
             @pl.when(owner == 0)
             def _():
@@ -429,11 +559,11 @@
             def _():
                 remote(obuf.at[slot], dbuf.at[w], out_sem.at[slot], in_sem.at[w], left).wait_send()
 
-            obuf[slot] = d_out.astype(jnp.bfloat16)
+            obuf[slot] = dyb[...].astype(jnp.bfloat16)
             dst = w + jnp.where(first, num_micro, 0)
             remote(obuf.at[slot], dbuf.at[dst], out_sem.at[slot], in_sem.at[dst], left).start()
 
-        y = (hr * gain).astype(jnp.bfloat16)
+        y = yb[...]
         for k in range(d_ff // step):
             rows = pl.ds(k * step, step)
             acc2[rows, :] += nt(hid_in[par, rows, :], d_in)
@@ -493,6 +623,7 @@
             pltpu.VMEM((2, d_model, tokens), bf), pltpu.VMEM((2, d_ff, tokens), f32), pltpu.VMEM((2, d_ff, tokens), bf),
             pltpu.VMEM((d_ff, tokens), bf), pltpu.VMEM((d_model, d_ff), f32), pltpu.VMEM((d_ff, d_model), f32), pltpu.VMEM((d_model, tokens), f32),
             pltpu.VMEM((d_model, d_ff), bf), pltpu.VMEM((d_ff, d_model), bf),
+            pltpu.VMEM((d_model, tokens), f32), pltpu.VMEM((d_model, tokens), f32), pltpu.VMEM((d_model, tokens), f32), pltpu.VMEM((d_model, tokens), bf),
             dma((n_unit,)), dma((per,)), dma((4,)), dma((4,)), dma((per,)), dma((2,)), dma((2,)), dma((2,)), dma((2,)),
         ],
         compiler_params=pltpu.CompilerParams(collective_id=1, has_side_effects=True, vmem_limit_bytes=VMEM_MAX),
@@ -507,8 +638,8 @@
         stage_id = lax.axis_index('pp')
         gains = jnp.swapaxes(norm_gain[0], 1, 2)
         w1, w2 = w_up[0, :, 0], w_down[0, :, 0]
-        saved, slope, hid, h_fin = run_forward(jnp.swapaxes(x_embed, 1, 2), gains, jnp.swapaxes(w1, 1, 2), jnp.swapaxes(w2, 1, 2), n_stage)
-        loss, head_grad, d_fin = run_head(h_fin, labels, w_head, stage_id, n_stage)
+        saved, slope, hid, h_fin, n_t, wt = run_forward(x_embed, gains, w1, w2, w_head, 3, n_stage)
+        loss, head_grad, d_fin = run_head(h_fin, n_t, wt, labels, w_head, stage_id, n_stage)
         dw1, dw2, dg, dx = run_backward(d_fin, saved, slope, hid, gains, w1, w2, n_stage)
         return (loss.reshape(1), jnp.swapaxes(dx, 1, 2), jnp.swapaxes(dg, 1, 2)[None], dw1[None, :, None], dw2[None, :, None], head_grad)
 

time: 816 us -> 754 us (0.924)
  local copies, waits for them, and re-layouts: 52.2 us -> 14 us
  Pallas kernels: 728 us -> 702 us
    pallas_call x1, Pallas kernels: 164 us -> 135 us  [run_head(): pl.pallas_call(functools.partial(logits_kernel, tile), name='head_logits'...]
    reshape x1 -> x0, local copies, waits for them, and re-layouts: 17.2 us -> none  [run_head(): wt = jnp.swapaxes(w_head.reshape(n_tile, tile, d_model), 1, 2)]
    transpose x2 -> x0, local copies, waits for them, and re-layouts: 12.4 us -> none  [the longest x1 6.2 us: local_step(): jnp.swapaxes(w1, 1, 2)]
    unnamed x16 -> x9, local copies, waits for them, and re-layouts: 19.5 us -> 10.8 us
where the time goes in v2:
time: 754 us; the launch traced here: 753 us
  Pallas kernels  702 us (93%)
  between operations  15.9 us (2%)
  local copies, waits for them, and re-layouts  14 us (2%)
  other arithmetic  12.5 us (2%)
  blocking collectives  8.83 us (1%)
    pallas_call x1, Pallas kernels, run_backward(): pl.pallas_call(functools.partial(bwd_kernel, n_stage, num_micro), name='s...  191 us
    pallas_call x1, Pallas kernels, run_forward(): pl.pallas_call(functools.partial(fwd_kernel, n_stage, num_micro), name='s...  179 us
    pallas_call x1, Pallas kernels, run_head(): pl.pallas_call(functools.partial(logits_kernel, tile), name='head_logits'...  135 us
    pallas_call x1, Pallas kernels, run_head(): pl.pallas_call(functools.partial(dnorm_kernel, inv), name='head_dnorm', g...  104 us
    pallas_call x1, Pallas kernels, run_head(): pl.pallas_call(functools.partial(dhead_kernel, inv), name='head_dweight',...  94.1 us
  transfers between devices with their start and end apart: 1, of which 0 were waited for; matrix products, arithmetic and copies ran while one was open for 0% of the time, Pallas kernels for 12%

profile of v2, /device:TPU:0, one launch (start us, length us, event | category | flops | bytes accessed | tf_op | source)
XLA Modules:
  0.0 753.1 jit_solution(13865236663117970755)
XLA Ops:
  7.2 0.0 reduce-scatter.4.cloned.1.call-start
  7.2 0.7 reduce.2
  7.9 1.0 transpose_squeeze.4.g_ref
  8.9 0.8 broadcast_subtract_fusion
  9.7 0.6 reshape.35.lab_ref
  10.3 178.5 %stack_fwd.1 = (bf16[24,512,512]{2,1,0:T(8,128)(2,1)}, f32[24,2048,512]{2,1,0:T(8,128)}, bf16[24,2048,512]{2,1,0:T(8,128)(2,1)}, bf16[12,512,512]{2,1,0:T(8,128)...) custom-call(bf16[12,512,512]{2,1,0:T(8,128)(2,1)} %x_ref.1, f32[2,512,1]{2,1,0:T(8,128)} %transpose_squeeze.4.g_ref, ...), custom_call_target="tpu_custom_call" | custom-call | flops 51539607552 | bytes 176160768 | tf_op jit(solution)/shard_map/stack_fwd/pallas_call | solution.py:213
  188.8 134.8 %head_logits.1 = (bf16[12,12576,512]{2,1,0:T(8,128)(2,1)}, f32[12,16,512]{2,1,0:T(8,128)}, f32[12,8,512]{2,1,0:T(8,128)}) custom-call(bf16[12,512,512]{2,1,0:T(8,128)(2,1)} %get-tuple-element.19.n_all.n_ref, s32[12,1,512]{2,1,0:T(1,128)} %reshape.35.lab_ref, bf16[12576,512]{1,0:T(8,128)(2,1)} %w_ref.1), custom_call_target="tpu_custom_call" | custom-call | flops 79121350656 | bytes 154533888 | tf_op jit(solution)/shard_map/head_logits/pallas_call | solution.py:397
  323.6 0.9 slice.12
  324.5 8.8 %all-gather = f32[48,3,512]{2,1,0:T(4,128)S(1)} all-gather(f32[12,3,512]{2,1,0:T(4,128)S(1)} %slice.12), channel_id=2, replica_groups=mesh['dp'=2,'pp'=4] {'pp'}, dimensions={0}, use_global_device_ids=true | all-gather | bytes 368640 | tf_op jit(solution)/shard_map/all_gather | solution.py:408
  333.4 0.3 fusion.11
  333.8 0.6 broadcast_divide_fusion
  334.4 1.8 exponential_multiply_fusion.fac_ref
  336.2 103.8 %head_dnorm.1 = f32[12,512,512]{2,1,0:T(8,128)} custom-call(bf16[12,12576,512]{2,1,0:T(8,128)(2,1)} %get-tuple-element.22.e_ref, f32[12,16,512]{2,1,0:T(8,128)} %exponential_multiply_fusion.fac_ref, s32[12,1,512]{2,1,0:T(1,128)} %reshape.35.lab_ref, bf16[3,512,4192]{2,1,0:T(8,128)(2,1)} %get-tuple-element.24.wt_ref), custom_call_target="tpu_custom_call" | custom-call | flops 79121350656 | bytes 154533888 | tf_op jit(solution)/shard_map/head_dnorm/pallas_call | solution.py:415
  440.0 0.0 reduce-scatter.4.cloned.1.call-update
  440.7 1.7 fusion.6
  442.5 94.1 %head_dweight.1 = bf16[12576,512]{1,0:T(8,128)(2,1)} custom-call(bf16[12,12576,512]{2,1,0:T(8,128)(2,1)} %get-tuple-element.22.e_ref, f32[12,16,512]{2,1,0:T(8,128)} %exponential_multiply_fusion.fac_ref, s32[12,1,512]{2,1,0:T(1,128)} %reshape.35.lab_ref, bf16[12,512,512]{2,1,0:T(8,128)(2,1)} %get-tuple-element.19.n_all.n_ref), custom_call_target="tpu_custom_call" | custom-call | flops 79121350656 | bytes 154533888 | tf_op jit(solution)/shard_map/head_dweight/pallas_call | solution.py:425
  536.5 0.0 reduce-scatter.4.cloned.1.call-done
  536.5 0.0 copy-start
  536.5 3.0 fusion.2
  539.6 0.3 copy-done
  539.8 3.3 fusion.5.dfin_ref
  543.1 190.6 %stack_bwd.1 = (bf16[2,512,2048]{2,1,0:T(8,128)(2,1)}, bf16[2,2048,512]{2,1,0:T(8,128)(2,1)}, f32[2,512,1]{2,1,0:T(8,128)}, f32[3,512,512]{2,1,0:T(8,128)}) custom-call(bf16[3,512,512]{2,1,0:T(8,128)(2,1)} %fusion.5.dfin_ref, bf16[24,512,512]{2,1,0:T(8,128)(2,1)} %get-tuple-element.25.saved_ref, f32[24,2048,512]{2,1,0:T(8,128)} %get-tuple-element.26.slope_ref, ...), custom_call_target="tpu_custom_call" | custom-call | flops 103079215104 | bytes 176160768 | tf_op jit(solution)/shard_map/stack_bwd/pallas_call | solution.py:614
  733.7 0.0 copy-start.2
  733.7 3.6 copy.36
  737.4 0.0 copy-done.2
  737.4 0.2 reduce.3
  737.6 0.6 broadcast_in_dim_transpose.4
  738.2 0.0 copy-start.1
  738.2 4.9 copy.61
  743.1 0.0 copy-done.1
  743.1 2.0 copy.62
  (3 shorter events, 0.1 us)
Async XLA Ops:
  7.2 529.4 %reduce-scatter.4.cloned.1.call-start = ((), (), s32[]{:S(2)}) async-start(), calls=%async_computation.1 | async-start | bytes 15728640
  536.5 3.3 copy-start
  733.7 3.6 copy-start.2
  738.2 4.9 copy-start.1
Sparse Core Ops, SparseCore 0:
  440.2 91.4 reduce-scatter.3

commit v3 on v2

--- a/solution.py
+++ b/solution.py
@@ -12,6 +12,7 @@
 GELU_A = 0.7978845608028654
 GELU_B = GELU_A * 0.044715
 SUB = 1024
+RANGE = 40.0
 
 ANY = pl.BlockSpec(memory_space=pl.ANY)
 VMEM = pl.BlockSpec(memory_space=pltpu.VMEM)
@@ -69,8 +70,8 @@
         last_sub = k + 1 == len(subs)
         src, dst = (wh_last, wht_last) if last_sub else (wh_in, wh_out)
         rows = pl.ds(pl.multiple_of(t * tile + off, 16), size)
-        return (src, dst, pltpu.make_async_copy(wh_ref.at[rows, :], src, whi_sem.at[int(last_sub)]),
-                pltpu.make_async_copy(dst, wht_ref.at[t, :, off:off + size], who_sem.at[int(last_sub)]))
+        return (src, dst, lambda: pltpu.make_async_copy(wh_ref.at[rows, :], src, whi_sem.at[int(last_sub)]),
+                lambda: pltpu.make_async_copy(dst, wht_ref.at[t, :, off:off + size], who_sem.at[int(last_sub)]))
 
     @pl.when(first)
     def _():
@@ -148,16 +149,17 @@
         for k in range(len(subs)):
             @pl.when((lax.rem(u, 2 * len(subs)) == 2 * k) & (u // (2 * len(subs)) < n_tile))
             def _(k=k):
-                head_copies(u // (2 * len(subs)), k)[2].start()
+                head_copies(u // (2 * len(subs)), k)[2]().start()
 
             @pl.when((lax.rem(u, 2 * len(subs)) == 2 * k + 1) & (u // (2 * len(subs)) < n_tile))
             def _(k=k):
                 t = u // (2 * len(subs))
                 src, dst, copy_in, copy_out = head_copies(t, k)
-                copy_in.wait()
+                copy_in().wait()
                 dst[...] = src[...].T
-                copy_out.start()
-                copy_out.wait()
+                copy = copy_out()
+                copy.start()
+                copy.wait()
 
     for slot in range(4):
         remote(obuf.at[slot], hbuf.at[0], out_sem.at[slot], in_sem.at[0], right).wait_send()
@@ -236,93 +238,64 @@
     return [(k * SUB, SUB if k + 1 < n_sub else tile - k * SUB) for k in range(n_sub)]
 
 
-def label_group(lab):
-    return jnp.where(lax.broadcasted_iota(jnp.int32, (8, lab.shape[1]), 0) == (lab & 7), lab >> 3, -1)
-
-
-def logits_kernel(tile, n_all, lab_ref, w_ref, e_ref, mrun_ref, stat_ref, z0, z1, run):
-    i = pl.program_id(0)
-    num_micro = pl.num_programs(0)
+def logits_kernel(tile, n_ref, lab_ref, w_ref, e_ref, mrun_ref, stat_ref, used, s_buf):
     vocab, tokens = e_ref.shape[1], e_ref.shape[2]
-    subs = sub_tiles(tile)
-    n_sub, n_tile = len(subs), vocab // tile
-    zbuf = (z0, z1)
-    piece = 256
-    low = jnp.full((8, tokens), -jnp.inf, jnp.float32)
+    n_tile = vocab // tile
+    piece, small = 256, 32
+    n = n_ref[0]
+    lab = lab_ref[0]
+    group = jnp.where(lax.broadcasted_iota(jnp.int32, (8, tokens), 0) == (lab & 7), lab >> 3, -1)
 
     def rows_at(t, off, size):
         return pl.ds(pl.multiple_of(t * tile + off, 16), size)
 
-    def dot_part(dst, t, off, size, base, n, group, top, hit):
-        z = nn(w_ref[rows_at(t, off, size), :], n)
-        dst[off - base:off - base + size, :] = z
-        for g in range(size // 8):
-            zg = z[g * 8:g * 8 + 8, :]
-            top = jnp.maximum(top, zg)
-            hit = jnp.where(group == t * (tile // 8) + (off // 8 + g), zg, hit)
-        return top, hit
-
-    def exp_part(src, t, base, lo, hi, m16, s8):
-        for r in range(lo, hi, 16):
-            e = jnp.exp(src[r:r + 16, :] - m16)
-            e_ref[0, rows_at(t, base + r, 16), :] = e.astype(jnp.bfloat16)
-            s8 = s8 + (e[0:8, :] + e[8:16, :])
-        return s8
-
-    def pieces(size):
-        n_piece = size // piece
-        return [(q * piece, piece if q + 1 < n_piece else size - q * piece) for q in range(n_piece)]
-
-    def first_dot(m):
-        n, group, top, hit = n_all[m], label_group(lab_ref[m]), low, jnp.zeros((8, tokens), jnp.float32)
-        return n, group, top, hit
-
-    def joint(kn, tn, n, group, top, hit, kc, tc, m, s8):
-        m16 = jnp.broadcast_to(m, (16, tokens))
-        base_n, size_n = subs[kn]
-        base_c, size_c = subs[kc]
-        parts = pieces(size_n)
-        cut = -(-size_c // (16 * len(parts))) * 16
-        for q, (off, size) in enumerate(parts):
-            top, hit = dot_part(zbuf[kn % 2], tn, base_n + off, size, base_n, n, group, top, hit)
-            s8 = exp_part(zbuf[kc % 2], tc, base_c, min(q * cut, size_c), min((q + 1) * cut, size_c), m16, s8)
-        return top, hit, s8
-
-    @pl.when(i == 0)
-    def _():
-        n, group, top, hit = first_dot(0)
-        for off, size in pieces(subs[0][1]):
-            top, hit = dot_part(z0, 0, off, size, 0, n, group, top, hit)
-        run[0:8, :] = top
-        run[8:16, :] = hit
-
-    n = n_all[i]
-    group = label_group(lab_ref[i])
-
-    def step(kn, tn, kc, tc, carry):
-        m, s8, hit = carry
-        top, hit, s8 = joint(kn, tn, n, group, low, hit, kc, tc, m, s8)
-        m_new = jnp.maximum(m, jnp.max(top, axis=0, keepdims=True))
-        mrun_ref[0, pl.ds(tn * n_sub + kn, 1), :] = m_new
-        return m_new, s8 * jnp.exp(m - m_new), hit
-
-    m = jnp.max(run[0:8, :], axis=0, keepdims=True)
-    mrun_ref[0, 0:1, :] = m
-    carry = (m, jnp.zeros((8, tokens), jnp.float32), run[8:16, :])
-
     def body(t, carry):
-        for k in range(n_sub):
-            carry = step((k + 1) % n_sub, t + (k + 1) // n_sub, k, t, carry)
-        return carry
-
-    carry = lax.fori_loop(0, n_tile - 1, body, carry)
-    for k in range(n_sub - 1):
-        carry = step(k + 1, n_tile - 1, k, n_tile - 1, carry)
-    m, s8, hit = carry
-    n2, group2, top2, hit2 = first_dot(jnp.minimum(i + 1, num_micro - 1))
-    top2, hit2, s8 = joint(0, 0, n2, group2, top2, hit2, n_sub - 1, n_tile - 1, m, s8)
-    run[0:8, :] = top2
-    run[8:16, :] = hit2
+        m_run, s_run, hit = carry
+        m_use = jnp.where(t == 0, 0.0, m_run)
+        m8 = jnp.broadcast_to(m_use, (8, tokens))
+        top = jnp.full((8, tokens), -jnp.inf, jnp.float32)
+        s8 = jnp.zeros((8, tokens), jnp.float32)
+        local = group - t * (tile // 8)
+        n_piece = tile // piece
+        for q in range(n_piece):
+            off = q * piece
+            size = piece if q + 1 < n_piece else tile - off
+            z = nn(w_ref[rows_at(t, off, size), :], n)
+            for r in range(0, size, 16):
+                e = []
+                for g in range(2):
+                    zg = z[r + 8 * g:r + 8 * g + 8, :]
+                    top = jnp.maximum(top, zg)
+                    hit = jnp.where(local == (off + r) // 8 + g, zg, hit)
+                    e.append(jnp.exp(zg - m8))
+                    s8 = s8 + e[g]
+                e_ref[0, rows_at(t, off + r, 16), :] = jnp.concatenate(e, axis=0).astype(jnp.bfloat16)
+        m_new = jnp.maximum(m_run, jnp.max(top, axis=0, keepdims=True))
+        used[0:1, :] = m_use
+        s_buf[...] = s8
+        rise = jnp.max(m_new - m_use)
+        fall = jnp.max(m_use - m_new)
+
+        @pl.when((rise > RANGE) | (fall > RANGE))
+        def _():
+            used[0:1, :] = m_new
+            s_buf[...] = jnp.zeros_like(s_buf)
+
+            @pl.loop(0, tile // small)
+            def _(q):
+                e = jnp.exp(nn(w_ref[rows_at(t, q * small, small), :], n) - m_new)
+                e_ref[0, rows_at(t, q * small, small), :] = e.astype(jnp.bfloat16)
+                for r in range(0, small, 8):
+                    s_buf[...] += e[r:r + 8, :]
+
+        m_use = used[0:1, :]
+        mrun_ref[0, pl.ds(t, 1), :] = m_use
+        s_run = s_run * jnp.exp(m_run - m_new) + s_buf[...] * jnp.exp(m_use - m_new)
+        return m_new, s_run, hit
+
+    low = jnp.full((1, tokens), -jnp.inf, jnp.float32)
+    zero = jnp.zeros((8, tokens), jnp.float32)
+    m, s8, hit = lax.fori_loop(0, n_tile, body, (low, zero, zero))
     stat_ref[0, 0:1, :] = m
     stat_ref[0, 1:2, :] = jnp.sum(s8, axis=0, keepdims=True)
     stat_ref[0, 2:3, :] = jnp.sum(hit, axis=0, keepdims=True)
@@ -340,7 +313,7 @@
     lab = lab_ref[0] - j * tile
     total = None
     for k, (off, size) in enumerate(subs):
-        d = d_logits(e_ref[0, off:off + size, :], fac_ref[0, pl.ds(j * len(subs) + k, 1), :], lab, off, inv)
+        d = d_logits(e_ref[0, off:off + size, :], fac_ref[0, pl.ds(j, 1), :], lab, off, inv)
         part = nn(wt_ref[j, :, off:off + size], d)
         total = part if total is None else total + part
 
@@ -366,7 +339,7 @@
     for k, (off, size) in enumerate(subs):
         total = None
         for b in range(per):
-            d = d_logits(e_ref[b, off:off + size, :], fac_ref[b, pl.ds(j * len(subs) + k, 1), :], lab_ref[b] - j * tile, off, inv)
+            d = d_logits(e_ref[b, off:off + size, :], fac_ref[b, pl.ds(j, 1), :], lab_ref[b] - j * tile, off, inv)
             part = nt(d, n_ref[b])
             total = part if total is None else total + part
         acc[off:off + size, :] += total
@@ -380,7 +353,7 @@
     num_micro, d_model, tokens = h_fin.shape
     vocab = w_head.shape[0]
     n_tile, tile = wt.shape[0], wt.shape[2]
-    n_row = 16
+    n_row = 8
     bf, f32 = jnp.bfloat16, jnp.float32
     inv = 1.0 / (num_micro * tokens)
     lab = (labels - stage_id * vocab).reshape(num_micro, 1, tokens)
@@ -393,15 +366,14 @@
     def micro2(shape):
         return pl.BlockSpec(shape, lambda i, j: (i, 0, 0))
 
-    z_rows = tile - (tile // SUB - 1) * SUB
     e, m_run, stat = pl.pallas_call(
         functools.partial(logits_kernel, tile), name="head_logits",
         grid=(num_micro,),
         out_shape=(jax.ShapeDtypeStruct((num_micro, vocab, tokens), bf), jax.ShapeDtypeStruct((num_micro, n_row, tokens), f32),
                    jax.ShapeDtypeStruct((num_micro, 8, tokens), f32)),
-        in_specs=[VMEM, VMEM, VMEM],
+        in_specs=[micro((1, d_model, tokens)), micro((1, 1, tokens)), VMEM],
         out_specs=(micro((1, vocab, tokens)), micro((1, n_row, tokens)), micro((1, 8, tokens))),
-        scratch_shapes=[pltpu.VMEM((z_rows, tokens), f32), pltpu.VMEM((z_rows, tokens), f32), pltpu.VMEM((16, tokens), f32)],
+        scratch_shapes=[pltpu.VMEM((8, tokens), f32), pltpu.VMEM((8, tokens), f32)],
         compiler_params=params, cost_estimate=cost,
     )(n_t, lab, w_head)
 
@@ -410,13 +382,13 @@
     m_top = jnp.max(m_all, axis=0)
     s_top = jnp.sum(s_all * jnp.exp(m_all - m_top), axis=0)
     loss = jnp.sum(m_top + jnp.log(s_top) - jnp.sum(stats[:, :, 2], axis=0)) * inv
-    fac = jnp.exp(m_run - m_top[:, None, :]) * (inv / s_top)[:, None, :]
+    fac = jnp.exp(m_run[:, :n_tile] - m_top[:, None, :]) * (inv / s_top)[:, None, :]
 
     dn = pl.pallas_call(
         functools.partial(dnorm_kernel, inv), name="head_dnorm",
         grid=(num_micro, n_tile),
         out_shape=jax.ShapeDtypeStruct((num_micro, d_model, tokens), f32),
-        in_specs=[pl.BlockSpec((1, tile, tokens), lambda i, j: (i, j, 0)), micro2((1, n_row, tokens)), micro2((1, 1, tokens)), VMEM],
+        in_specs=[pl.BlockSpec((1, tile, tokens), lambda i, j: (i, j, 0)), micro2((1, n_tile, tokens)), micro2((1, 1, tokens)), VMEM],
         out_specs=micro2((1, d_model, tokens)),
         compiler_params=params, cost_estimate=cost,
     )(e, fac, lab, wt)
@@ -426,7 +398,7 @@
         functools.partial(dhead_kernel, inv), name="head_dweight",
         grid=(n_tile, num_micro // per),
         out_shape=jax.ShapeDtypeStruct((vocab, d_model), bf),
-        in_specs=[pl.BlockSpec((per, tile, tokens), lambda j, i: (i, j, 0)), pl.BlockSpec((per, n_row, tokens), lambda j, i: (i, 0, 0)),
+        in_specs=[pl.BlockSpec((per, tile, tokens), lambda j, i: (i, j, 0)), pl.BlockSpec((per, n_tile, tokens), lambda j, i: (i, 0, 0)),
                   pl.BlockSpec((per, 1, tokens), lambda j, i: (i, 0, 0)), pl.BlockSpec((per, d_model, tokens), lambda j, i: (i, 0, 0))],
         out_specs=pl.BlockSpec((tile, d_model), lambda j, i: (j, 0)),
         scratch_shapes=[pltpu.VMEM((tile, d_model), f32)],
@@ -541,7 +513,7 @@
             def _():
                 remote(xbuf.at[slot], dx_ref.at[0], x_sem.at[slot], xr_sem.at[0], left).wait_send()
 
-            xbuf[slot] = dyb[...]
+            xbuf[slot] = dyb[...].astype(jnp.bfloat16)
 
             @pl.when(owner == 0)
             def _():
@@ -615,11 +587,11 @@
         functools.partial(bwd_kernel, n_stage, num_micro),
         name="stack_bwd",
         out_shape=(jax.ShapeDtypeStruct(w1.shape, bf), jax.ShapeDtypeStruct(w2.shape, bf), jax.ShapeDtypeStruct((2, d_model, 1), f32),
-                   jax.ShapeDtypeStruct((per, d_model, tokens), f32)),
+                   jax.ShapeDtypeStruct((per, d_model, tokens), bf)),
         in_specs=[ANY, ANY, ANY, ANY, VMEM, VMEM, VMEM],
         out_specs=(ANY, ANY, VMEM, ANY),
         scratch_shapes=[
-            pltpu.VMEM((n_unit, d_model, tokens), bf), pltpu.VMEM((4, d_model, tokens), bf), pltpu.VMEM((4, d_model, tokens), f32),
+            pltpu.VMEM((n_unit, d_model, tokens), bf), pltpu.VMEM((4, d_model, tokens), bf), pltpu.VMEM((4, d_model, tokens), bf),
             pltpu.VMEM((2, d_model, tokens), bf), pltpu.VMEM((2, d_ff, tokens), f32), pltpu.VMEM((2, d_ff, tokens), bf),
             pltpu.VMEM((d_ff, tokens), bf), pltpu.VMEM((d_model, d_ff), f32), pltpu.VMEM((d_ff, d_model), f32), pltpu.VMEM((d_model, tokens), f32),
             pltpu.VMEM((d_model, d_ff), bf), pltpu.VMEM((d_ff, d_model), bf),
@@ -641,7 +613,7 @@
         saved, slope, hid, h_fin, n_t, wt = run_forward(x_embed, gains, w1, w2, w_head, 3, n_stage)
         loss, head_grad, d_fin = run_head(h_fin, n_t, wt, labels, w_head, stage_id, n_stage)
         dw1, dw2, dg, dx = run_backward(d_fin, saved, slope, hid, gains, w1, w2, n_stage)
-        return (loss.reshape(1), jnp.swapaxes(dx, 1, 2), jnp.swapaxes(dg, 1, 2)[None], dw1[None, :, None], dw2[None, :, None], head_grad)
+        return (loss.reshape(1), jnp.swapaxes(dx, 1, 2).astype(jnp.float32), jnp.swapaxes(dg, 1, 2)[None], dw1[None, :, None], dw2[None, :, None], head_grad)
 
     part_spec = P('dp')
     stage_spec = P('pp')

time: 754 us -> 708 us (0.939)
  Pallas kernels: 702 us -> 654 us
    pallas_call x1, Pallas kernels: 191 us -> 165 us  [run_backward(): pl.pallas_call(functools.partial(bwd_kernel, n_stage, num_micro), name='s...]
    pallas_call x1, Pallas kernels: 135 us -> 112 us  [run_head(): pl.pallas_call(functools.partial(logits_kernel, tile), name='head_logits'...]
  transfers between devices with their start and end apart: 1 -> 1, of which waited for: 0 -> 0; matrix products, arithmetic and copies ran while one was open for 0% -> 0% of each run, Pallas kernels for 12% -> 13%
where the time goes in v3:
time: 708 us; the launch traced here: 707 us
  Pallas kernels  654 us (92%)
  between operations  15.9 us (2%)
  other arithmetic  15.2 us (2%)
  local copies, waits for them, and re-layouts  12.7 us (2%)
  blocking collectives  8.79 us (1%)
    pallas_call x1, Pallas kernels, run_forward(): pl.pallas_call(functools.partial(fwd_kernel, n_stage, num_micro), name='s...  179 us
    pallas_call x1, Pallas kernels, run_backward(): pl.pallas_call(functools.partial(bwd_kernel, n_stage, num_micro), name='s...  165 us
    pallas_call x1, Pallas kernels, run_head(): pl.pallas_call(functools.partial(logits_kernel, tile), name='head_logits'...  112 us
    pallas_call x1, Pallas kernels, run_head(): pl.pallas_call(functools.partial(dnorm_kernel, inv), name='head_dnorm', g...  104 us
    pallas_call x1, Pallas kernels, run_head(): pl.pallas_call(functools.partial(dhead_kernel, inv), name='head_dweight',...  94.1 us
  transfers between devices with their start and end apart: 1, of which 0 were waited for; matrix products, arithmetic and copies ran while one was open for 0% of the time, Pallas kernels for 13%

profile of v3, /device:TPU:0, one launch (start us, length us, event | category | flops | bytes accessed | tf_op | source)
XLA Modules:
  0.0 707.1 jit_solution(1438066391181071765)
XLA Ops:
  7.2 0.0 reduce-scatter.4.cloned.1.call-start
  7.2 0.7 reduce.2
  7.9 1.0 transpose_squeeze.4.g_ref
  8.9 0.8 broadcast_subtract_fusion
  9.7 0.6 reshape.35.lab_ref
  10.3 178.5 %stack_fwd.1 = (bf16[24,512,512]{2,1,0:T(8,128)(2,1)}, f32[24,2048,512]{2,1,0:T(8,128)}, bf16[24,2048,512]{2,1,0:T(8,128)(2,1)}, bf16[12,512,512]{2,1,0:T(8,128)...) custom-call(bf16[12,512,512]{2,1,0:T(8,128)(2,1)} %x_ref.1, f32[2,512,1]{2,1,0:T(8,128)} %transpose_squeeze.4.g_ref, ...), custom_call_target="tpu_custom_call" | custom-call | flops 51539607552 | bytes 176160768 | tf_op jit(solution)/shard_map/stack_fwd/pallas_call | solution.py:215
  188.8 112.2 %head_logits.1 = (bf16[12,12576,512]{2,1,0:T(8,128)(2,1)}, f32[12,8,512]{2,1,0:T(8,128)}, f32[12,8,512]{2,1,0:T(8,128)}) custom-call(bf16[12,512,512]{2,1,0:T(8,128)(2,1)} %get-tuple-element.19.n_ref, s32[12,1,512]{2,1,0:T(1,128)} %reshape.35.lab_ref, bf16[12576,512]{1,0:T(8,128)(2,1)} %w_ref.1), custom_call_target="tpu_custom_call" | custom-call | flops 79121350656 | bytes 154533888 | tf_op jit(solution)/shard_map/head_logits/pallas_call | solution.py:369
  301.0 0.9 slice.15
  302.0 8.8 %all-gather = f32[48,3,512]{2,1,0:T(4,128)S(1)} all-gather(f32[12,3,512]{2,1,0:T(4,128)S(1)} %slice.15), channel_id=2, replica_groups=mesh['dp'=2,'pp'=4] {'pp'}, dimensions={0}, use_global_device_ids=true | all-gather | bytes 368640 | tf_op jit(solution)/shard_map/all_gather | solution.py:380
  310.8 0.3 fusion.11
  311.1 0.6 broadcast_divide_fusion
  311.8 1.6 exponential_multiply_fusion.fac_ref
  313.4 104.1 %head_dnorm.1 = f32[12,512,512]{2,1,0:T(8,128)} custom-call(bf16[12,12576,512]{2,1,0:T(8,128)(2,1)} %get-tuple-element.22.e_ref, f32[12,3,512]{2,1,0:T(4,128)} %exponential_multiply_fusion.fac_ref, s32[12,1,512]{2,1,0:T(1,128)} %reshape.35.lab_ref, bf16[3,512,4192]{2,1,0:T(8,128)(2,1)} %get-tuple-element.24.wt_ref), custom_call_target="tpu_custom_call" | custom-call | flops 79121350656 | bytes 154533888 | tf_op jit(solution)/shard_map/head_dnorm/pallas_call | solution.py:387
  417.5 0.0 reduce-scatter.4.cloned.1.call-update
  418.2 1.7 fusion.6
  419.9 94.1 %head_dweight.1 = bf16[12576,512]{1,0:T(8,128)(2,1)} custom-call(bf16[12,12576,512]{2,1,0:T(8,128)(2,1)} %get-tuple-element.22.e_ref, f32[12,3,512]{2,1,0:T(4,128)} %exponential_multiply_fusion.fac_ref, s32[12,1,512]{2,1,0:T(1,128)} %reshape.35.lab_ref, bf16[12,512,512]{2,1,0:T(8,128)(2,1)} %get-tuple-element.19.n_ref), custom_call_target="tpu_custom_call" | custom-call | flops 79121350656 | bytes 154533888 | tf_op jit(solution)/shard_map/head_dweight/pallas_call | solution.py:397
  514.0 0.0 reduce-scatter.4.cloned.1.call-done
  514.1 0.0 copy-start
  514.1 3.0 fusion.2
  517.1 0.3 copy-done
  517.4 3.3 fusion.5.dfin_ref
  520.6 165.4 %stack_bwd.1 = (bf16[2,512,2048]{2,1,0:T(8,128)(2,1)}, bf16[2,2048,512]{2,1,0:T(8,128)(2,1)}, f32[2,512,1]{2,1,0:T(8,128)}, bf16[3,512,512]{2,1,0:T(8,128)(2,1)}) custom-call(bf16[3,512,512]{2,1,0:T(8,128)(2,1)} %fusion.5.dfin_ref, bf16[24,512,512]{2,1,0:T(8,128)(2,1)} %get-tuple-element.25.saved_ref, f32[24,2048,512]{2,1,0:T(8,128)} %get-tuple-element.26.slope_ref, ...), custom_call_target="tpu_custom_call" | custom-call | flops 103079215104 | bytes 176160768 | tf_op jit(solution)/shard_map/stack_bwd/pallas_call | solution.py:586
  686.0 1.8 convert_bitcast_fusion
  687.9 2.4 copy.36
  690.3 1.2 reduce.3
  691.5 0.6 broadcast_in_dim_transpose.4
  692.1 0.0 copy-start.1
  692.1 4.9 copy.61
  697.1 0.0 copy-done.1
  697.1 2.0 copy.62
  (3 shorter events, 0.1 us)
Async XLA Ops:
  7.2 506.9 %reduce-scatter.4.cloned.1.call-start = ((), (), s32[]{:S(2)}) async-start(), calls=%async_computation.1 | async-start | bytes 15728640
  514.1 3.3 copy-start
  692.1 4.9 copy-start.1
Sparse Core Ops, SparseCore 0:
  417.7 91.4 reduce-scatter.3

commit v4 on v3

--- a/solution.py
+++ b/solution.py
@@ -156,11 +156,17 @@
                 t = u // (2 * len(subs))
                 src, dst, copy_in, copy_out = head_copies(t, k)
                 copy_in().wait()
+                if k in (0, len(subs) - 1):
+                    @pl.when(t > 0)
+                    def _():
+                        copy_out().wait()
+                else:
+                    copy_out().wait()
                 dst[...] = src[...].T
-                copy = copy_out()
-                copy.start()
-                copy.wait()
-
+                copy_out().start()
+
+    for k in (0, len(subs) - 1):
+        head_copies(0, k)[3]().wait()
     for slot in range(4):
         remote(obuf.at[slot], hbuf.at[0], out_sem.at[slot], in_sem.at[0], right).wait_send()
     for par in range(2):
@@ -414,16 +420,24 @@
     return loss, head_grad, d_fin.astype(bf)
 
 
-def bwd_kernel(n_stage, num_micro, dfin_ref, saved_ref, slope_ref, hid_ref, g_ref, w1_ref, w2_ref, dw1_ref, dw2_ref, dg_ref, dx_ref,
-               dbuf, obuf, xbuf, h_in, slope_in, hid_in, dpre, acc1, acc2, accg, st1, st2, gb, hrb, dyb, yb,
-               in_sem, push_sem, out_sem, x_sem, xr_sem, h_sem, slope_sem, hid_sem, w_sem):
+def bwd_kernel(n_stage, num_micro, dfin_ref, saved_ref, slope_ref, hid_ref, g_ref, w1_hbm, w2_hbm, dw1_ref, dw2_ref, dg_ref, dx_ref,
+               dbuf, obuf, xbuf, h_in, slope_in, hid_in, dpre, acc1, acc2, accg, st1, st2, gb, hrb, dyb, yb, w1_ref, w2_ref,
+               in_sem, push_sem, out_sem, x_sem, xr_sem, h_sem, slope_sem, hid_sem, w_sem, wl_sem):
     me = lax.axis_index("pp")
     left = lax.rem(me + n_stage - 1, n_stage)
     first, last = me == 0, me == n_stage - 1
     n_unit = 2 * num_micro
     per = num_micro // n_stage
     d_model, d_ff = w1_ref.shape[1:]
-    step = 512
+    step = 1024
+
+    def weights(half):
+        return (pltpu.make_async_copy(w1_hbm.at[half], w1_ref.at[half], wl_sem.at[half, 0]),
+                pltpu.make_async_copy(w2_hbm.at[half], w2_ref.at[half], wl_sem.at[half, 1]))
+
+    for half in (1, 0):
+        for copy in weights(half):
+            copy.start()
     group_barrier(me, n_stage)
 
     def fetch(w):
@@ -464,6 +478,8 @@
             acc1[...] = jnp.zeros_like(acc1)
             acc2[...] = jnp.zeros_like(acc2)
             accg[...] = jnp.zeros_like(accg)
+            for copy in weights(half):
+                copy.wait()
             gb[...] = jnp.broadcast_to(g_ref[half], gb.shape)
 
         @pl.when(is_local)
@@ -535,11 +551,8 @@
             dst = w + jnp.where(first, num_micro, 0)
             remote(obuf.at[slot], dbuf.at[dst], out_sem.at[slot], in_sem.at[dst], left).start()
 
-        y = yb[...]
-        for k in range(d_ff // step):
-            rows = pl.ds(k * step, step)
-            acc2[rows, :] += nt(hid_in[par, rows, :], d_in)
-            acc1[:, rows] += nt(y, dpre[rows, :])
+        acc2[...] += nt(hid_in[par], d_in)
+        acc1[...] += nt(dpre[...], yb[...])
 
         @pl.when(lax.rem(w, num_micro) == num_micro - 1)
         def _():
@@ -548,7 +561,7 @@
                 pltpu.make_async_copy(st1, dw1_ref.at[1], w_sem.at[0]).wait()
                 pltpu.make_async_copy(st2, dw2_ref.at[1], w_sem.at[1]).wait()
 
-            st1[...] = acc1[...].astype(jnp.bfloat16)
+            st1[...] = acc1[...].astype(jnp.bfloat16).T
             st2[...] = acc2[...].astype(jnp.bfloat16)
             dg_ref[half] = jnp.sum(accg[...], axis=1, keepdims=True)
             pltpu.make_async_copy(st1, dw1_ref.at[half], w_sem.at[0]).start()
@@ -588,15 +601,16 @@
         name="stack_bwd",
         out_shape=(jax.ShapeDtypeStruct(w1.shape, bf), jax.ShapeDtypeStruct(w2.shape, bf), jax.ShapeDtypeStruct((2, d_model, 1), f32),
                    jax.ShapeDtypeStruct((per, d_model, tokens), bf)),
-        in_specs=[ANY, ANY, ANY, ANY, VMEM, VMEM, VMEM],
+        in_specs=[ANY, ANY, ANY, ANY, VMEM, ANY, ANY],
         out_specs=(ANY, ANY, VMEM, ANY),
         scratch_shapes=[
             pltpu.VMEM((n_unit, d_model, tokens), bf), pltpu.VMEM((4, d_model, tokens), bf), pltpu.VMEM((4, d_model, tokens), bf),
             pltpu.VMEM((2, d_model, tokens), bf), pltpu.VMEM((2, d_ff, tokens), f32), pltpu.VMEM((2, d_ff, tokens), bf),
-            pltpu.VMEM((d_ff, tokens), bf), pltpu.VMEM((d_model, d_ff), f32), pltpu.VMEM((d_ff, d_model), f32), pltpu.VMEM((d_model, tokens), f32),
+            pltpu.VMEM((d_ff, tokens), bf), pltpu.VMEM((d_ff, d_model), f32), pltpu.VMEM((d_ff, d_model), f32), pltpu.VMEM((d_model, tokens), f32),
             pltpu.VMEM((d_model, d_ff), bf), pltpu.VMEM((d_ff, d_model), bf),
             pltpu.VMEM((d_model, tokens), f32), pltpu.VMEM((d_model, tokens), f32), pltpu.VMEM((d_model, tokens), f32), pltpu.VMEM((d_model, tokens), bf),
-            dma((n_unit,)), dma((per,)), dma((4,)), dma((4,)), dma((per,)), dma((2,)), dma((2,)), dma((2,)), dma((2,)),
+            pltpu.VMEM(w1.shape, bf), pltpu.VMEM(w2.shape, bf),
+            dma((n_unit,)), dma((per,)), dma((4,)), dma((4,)), dma((per,)), dma((2,)), dma((2,)), dma((2,)), dma((2,)), dma((2, 2)),
         ],
         compiler_params=pltpu.CompilerParams(collective_id=1, has_side_effects=True, vmem_limit_bytes=VMEM_MAX),
         cost_estimate=pl.CostEstimate(flops=8 * n_unit * tokens * d_model * d_ff, bytes_accessed=7 * n_unit * d_ff * tokens, transcendentals=0),

time: 708 us -> 704 us (level)
  no operation moved by 1% of the time
where the time goes in v4:
time: 704 us; the launch traced here: 703 us
  Pallas kernels  651 us (92%)
  between operations  15.9 us (2%)
  other arithmetic  15.2 us (2%)
  local copies, waits for them, and re-layouts  12.7 us (2%)
  blocking collectives  8.79 us (1%)
    pallas_call x1, Pallas kernels, run_forward(): pl.pallas_call(functools.partial(fwd_kernel, n_stage, num_micro), name='s...  177 us
    pallas_call x1, Pallas kernels, run_backward(): pl.pallas_call(functools.partial(bwd_kernel, n_stage, num_micro), name='s...  163 us
    pallas_call x1, Pallas kernels, run_head(): pl.pallas_call(functools.partial(logits_kernel, tile), name='head_logits'...  112 us
    pallas_call x1, Pallas kernels, run_head(): pl.pallas_call(functools.partial(dnorm_kernel, inv), name='head_dnorm', g...  104 us
    pallas_call x1, Pallas kernels, run_head(): pl.pallas_call(functools.partial(dhead_kernel, inv), name='head_dweight',...  94.1 us
  transfers between devices with their start and end apart: 1, of which 0 were waited for; matrix products, arithmetic and copies ran while one was open for 0% of the time, Pallas kernels for 13%

profile of v4, /device:TPU:0, one launch (start us, length us, event | category | flops | bytes accessed | tf_op | source)
XLA Modules:
  0.0 703.3 jit_solution(4607526756464626726)
XLA Ops:
  7.2 0.0 reduce-scatter.4.cloned.1.call-start
  7.2 0.7 reduce.2
  7.9 1.0 transpose_squeeze.4.g_ref
  8.9 0.8 broadcast_subtract_fusion
  9.7 0.6 reshape.35.lab_ref
  10.3 177.0 %stack_fwd.1 = (bf16[24,512,512]{2,1,0:T(8,128)(2,1)}, f32[24,2048,512]{2,1,0:T(8,128)}, bf16[24,2048,512]{2,1,0:T(8,128)(2,1)}, bf16[12,512,512]{2,1,0:T(8,128)...) custom-call(bf16[12,512,512]{2,1,0:T(8,128)(2,1)} %x_ref.1, f32[2,512,1]{2,1,0:T(8,128)} %transpose_squeeze.4.g_ref, ...), custom_call_target="tpu_custom_call" | custom-call | flops 51539607552 | bytes 176160768 | tf_op jit(solution)/shard_map/stack_fwd/pallas_call | solution.py:221
  187.3 112.2 %head_logits.1 = (bf16[12,12576,512]{2,1,0:T(8,128)(2,1)}, f32[12,8,512]{2,1,0:T(8,128)}, f32[12,8,512]{2,1,0:T(8,128)}) custom-call(bf16[12,512,512]{2,1,0:T(8,128)(2,1)} %get-tuple-element.19.n_ref, s32[12,1,512]{2,1,0:T(1,128)} %reshape.35.lab_ref, bf16[12576,512]{1,0:T(8,128)(2,1)} %w_ref.1), custom_call_target="tpu_custom_call" | custom-call | flops 79121350656 | bytes 154533888 | tf_op jit(solution)/shard_map/head_logits/pallas_call | solution.py:375
  299.5 0.9 slice.15
  300.5 8.8 %all-gather = f32[48,3,512]{2,1,0:T(4,128)S(1)} all-gather(f32[12,3,512]{2,1,0:T(4,128)S(1)} %slice.15), channel_id=2, replica_groups=mesh['dp'=2,'pp'=4] {'pp'}, dimensions={0}, use_global_device_ids=true | all-gather | bytes 368640 | tf_op jit(solution)/shard_map/all_gather | solution.py:386
  309.3 0.3 fusion.11
  309.7 0.6 broadcast_divide_fusion
  310.3 1.6 exponential_multiply_fusion.fac_ref
  311.9 104.1 %head_dnorm.1 = f32[12,512,512]{2,1,0:T(8,128)} custom-call(bf16[12,12576,512]{2,1,0:T(8,128)(2,1)} %get-tuple-element.22.e_ref, f32[12,3,512]{2,1,0:T(4,128)} %exponential_multiply_fusion.fac_ref, s32[12,1,512]{2,1,0:T(1,128)} %reshape.35.lab_ref, bf16[3,512,4192]{2,1,0:T(8,128)(2,1)} %get-tuple-element.24.wt_ref), custom_call_target="tpu_custom_call" | custom-call | flops 79121350656 | bytes 154533888 | tf_op jit(solution)/shard_map/head_dnorm/pallas_call | solution.py:393
  416.0 0.0 reduce-scatter.4.cloned.1.call-update
  416.7 1.7 fusion.6
  418.5 94.1 %head_dweight.1 = bf16[12576,512]{1,0:T(8,128)(2,1)} custom-call(bf16[12,12576,512]{2,1,0:T(8,128)(2,1)} %get-tuple-element.22.e_ref, f32[12,3,512]{2,1,0:T(4,128)} %exponential_multiply_fusion.fac_ref, s32[12,1,512]{2,1,0:T(1,128)} %reshape.35.lab_ref, bf16[12,512,512]{2,1,0:T(8,128)(2,1)} %get-tuple-element.19.n_ref), custom_call_target="tpu_custom_call" | custom-call | flops 79121350656 | bytes 154533888 | tf_op jit(solution)/shard_map/head_dweight/pallas_call | solution.py:403
  512.6 0.0 reduce-scatter.4.cloned.1.call-done
  512.6 0.0 copy-start
  512.6 3.0 fusion.2
  515.6 0.3 copy-done
  515.9 3.3 fusion.5.dfin_ref
  519.1 163.2 %stack_bwd.1 = (bf16[2,512,2048]{2,1,0:T(8,128)(2,1)}, bf16[2,2048,512]{2,1,0:T(8,128)(2,1)}, f32[2,512,1]{2,1,0:T(8,128)}, bf16[3,512,512]{2,1,0:T(8,128)(2,1)}) custom-call(bf16[3,512,512]{2,1,0:T(8,128)(2,1)} %fusion.5.dfin_ref, bf16[24,512,512]{2,1,0:T(8,128)(2,1)} %get-tuple-element.25.saved_ref, f32[24,2048,512]{2,1,0:T(8,128)} %get-tuple-element.26.slope_ref, ...), custom_call_target="tpu_custom_call" | custom-call | flops 103079215104 | bytes 176160768 | tf_op jit(solution)/shard_map/stack_bwd/pallas_call | solution.py:599
  682.3 1.8 convert_bitcast_fusion
  684.2 2.4 copy.36
  686.5 1.2 reduce.3
  687.8 0.6 broadcast_in_dim_transpose.4
  688.4 0.0 copy-start.1
  688.4 4.9 copy.61
  693.3 0.0 copy-done.1
  693.3 2.0 copy.62
  (3 shorter events, 0.1 us)
Async XLA Ops:
  7.2 505.4 %reduce-scatter.4.cloned.1.call-start = ((), (), s32[]{:S(2)}) async-start(), calls=%async_computation.1 | async-start | bytes 15728640
  512.6 3.3 copy-start
  688.4 4.9 copy-start.1
Sparse Core Ops, SparseCore 0:
  416.2 91.4 reduce-scatter.3
